TPU v7x, 256 devices: a whole 4x4x8 slice. The times are simulated.
256 devices in a mesh: row: 8 (over z_hi, core), col: 8 (over y, z_lo), dp: 4 (over x).
Axes of the slice: x: 4, y: 4, z: 8 (z_hi: 4, z_lo: 2; z = z_hi * 2 + z_lo), core: 2. Of those that a mesh axis runs over, the one named last changes fastest.
Arguments:
- inputs: bfloat16 [4096, 4096], P('dp', 'row'), may hold values from -6 to 6
- upstream: bfloat16 [4096, 4096], P('dp', 'row'), may hold values from -6 to 6
- expand: bfloat16 [4096, 16384], P('row', 'col'), may hold values from -0.09375 to 0.09375
- biases: float32 [16384], P('col'), may hold values from -5 to 5
- contract: bfloat16 [16384, 4096], P('col', 'row'), may hold values from -0.046875 to 0.046875
Outputs:
- grad_inputs: bfloat16 [4096, 4096], P('dp', 'row')
- grad_expand: bfloat16 [4096, 16384], P('row', 'col')
- grad_biases: bfloat16 [16384], P('col')
- grad_contract: bfloat16 [16384, 4096], P('col', 'row')
- grad_offset: bfloat16 [4096], P('row')
All inputs are finite; a program needn't handle non-finite values.
Results may differ from a plain program's by a relative error of at most 0.022.
Values may be sent and summed in bfloat16 or wider, within the bound.
A program may use at most 128 MiB of HBM per device.

v0:
```python
import jax
import jax.numpy as jnp
from jax import lax
from jax.sharding import PartitionSpec as P


def side_by_side(arrays, axis, dim, along):
    widths = [a.shape[along] for a in arrays]
    both = jnp.concatenate(arrays, axis=along)
    whole = lax.all_gather(both, axis, axis=dim, tiled=True)
    return tuple(jnp.split(whole, [sum(widths[:k]) for k in range(1, len(widths))], axis=along))


def gelu_tanh(values):
    return jax.nn.gelu(values, approximate=True)


def pointwise(hidden, backward):
    forward_act, pullback = jax.vjp(gelu_tanh, hidden.astype(jnp.float32))
    (slope_grad,) = pullback(backward.astype(jnp.float32))
    return (forward_act.astype(jnp.bfloat16), slope_grad.astype(jnp.bfloat16))


def back_product(upstream_rows, contract):
    return lax.dot_general(
        upstream_rows, contract, (((1,), (1,)), ((), ())), preferred_element_type=jnp.float32
    )


def local(inputs, upstream, expand, biases, contract):
    tok_rows = inputs.shape[0]
    factor = (tok_rows * lax.axis_size("dp")) ** (-0.5)
    row_block = inputs
    pre_share = lax.psum_scatter(
        jnp.dot(row_block, expand, preferred_element_type=jnp.float32).astype(jnp.bfloat16),
        "row",
        scatter_dimension=0,
        tiled=True,
    ).astype(jnp.float32)
    row_block = upstream
    back_share = lax.psum_scatter(
        back_product(row_block, contract).astype(jnp.bfloat16),
        "row",
        scatter_dimension=0,
        tiled=True,
    )
    hidden = (pre_share + biases[None, :]).astype(jnp.bfloat16)
    local_active, local_grad = pointwise(hidden, back_share)
    activation, hidden_grad = side_by_side((local_active, local_grad), "row", 0, 1)
    input_part = lax.dot_general(
        hidden_grad, expand, (((1,), (1,)), ((), ())), preferred_element_type=jnp.float32
    )
    grad_inputs = lax.psum(input_part.astype(jnp.bfloat16), "col")
    expand_part = (
        lax.dot_general(
            inputs, hidden_grad, (((0,), (0,)), ((), ())), preferred_element_type=jnp.float32
        )
        * factor
    )
    biases_part = jnp.sum(hidden_grad, axis=0, dtype=jnp.float32) * factor
    contract_part = (
        lax.dot_general(
            activation, upstream, (((0,), (0,)), ((), ())), preferred_element_type=jnp.float32
        )
        * factor
    )
    offset_part = jnp.sum(upstream, axis=0, dtype=jnp.float32) * factor
    reduced = (
        lax.psum(expand_part.astype(jnp.bfloat16), "dp").astype(jnp.float32),
        lax.psum(biases_part.astype(jnp.bfloat16), "dp").astype(jnp.float32),
        lax.psum(contract_part.astype(jnp.bfloat16), "dp").astype(jnp.float32),
        lax.psum(offset_part.astype(jnp.bfloat16), "dp").astype(jnp.float32),
    )
    return (
        grad_inputs,
        reduced[0].astype(jnp.bfloat16),
        reduced[1].astype(jnp.bfloat16),
        reduced[2].astype(jnp.bfloat16),
        reduced[3].astype(jnp.bfloat16),
    )


def solution(mesh):
    in_specs = (P("dp", "row"), P("dp", "row"), P("row", "col"), P("col"), P("col", "row"))
    out_specs = (P("dp", "row"), P("row", "col"), P("col"), P("col", "row"), P("row"))
    return jax.shard_map(local, mesh=mesh, in_specs=in_specs, out_specs=out_specs, check_vma=False)
```

profile of v0, /device:TPU:8, one launch (start us, length us, event | category | flops | bytes accessed | tf_op | source)
XLA Modules:
  0.0 432.4 jit_solution(5506745162084194373)
XLA Ops:
  7.2 0.0 reduce-scatter.5.cloned.1.call-start
  7.2 6.4 %convolution_convert_fusion = bf16[1024,2048]{1,0:T(8,128)(2,1)} fusion(bf16[1024,512]{1,0:T(8,128)(2,1)} %param.6, bf16[2048,512]{1,0:T(8,128)(2,1)} %param.9), kind=kOutput, calls=%fused_computation.5 | convolution fusion | flops 2149580800 | bytes 7340032 | tf_op jit(solution)/shard_map/dot_general | solution.py:25
  13.6 0.0 reduce-scatter.3.cloned.1.call-start
  13.7 1.1 copy-done.4
  14.8 4.3 convolution_convert_fusion.1
  19.1 0.0 all-gather.2.cloned.1.call-start
  19.2 54.1 %reduce-scatter.5.cloned.1.call-done = bf16[128,2048]{1,0:T(8,128)(2,1)} async-done(((bf16[1024,2048]{1,0:T(8,128)(2,1)}), bf16[128,2048]{1,0:T(8,128)(2,1)}) %reduce-scatter.5.cloned.1.call-update) | async-done | bytes 524304 | tf_op jit(solution)/shard_map/reduce_scatter | solution.py:41
  73.3 61.1 %reduce-scatter.3.cloned.1.call-done = bf16[128,2048]{1,0:T(8,128)(2,1)} async-done(((bf16[1024,2048]{1,0:T(8,128)(2,1)}), bf16[128,2048]{1,0:T(8,128)(2,1)}) %reduce-scatter.3.cloned.1.call-update) | async-done | bytes 524304 | tf_op jit(solution)/shard_map/reduce_scatter | solution.py:34
  134.4 2.1 fusion.21
  136.5 1.1 pad_maximum_fusion
  137.6 0.0 all-reduce.7.cloned.1.call-start
  137.7 85.6 %all-gather.2.cloned.1.call-done = bf16[1024,4096]{1,0:T(8,128)(2,1)} async-done(((bf16[128,4096]{1,0:T(8,128)(2,1)}), bf16[1024,4096]{1,0:T(8,128)(2,1)}) %all-gather.2.cloned.1.call-update) | async-done | bytes 8388624 | tf_op jit(solution)/shard_map/all_gather | solution.py:10
  223.2 6.3 %fusion.7 = bf16[512,2048]{0,1:T(8,128)(2,1)} fusion(bf16[1024,512]{1,0:T(8,128)(2,1)} %param.5, bf16[1024,4096]{1,0:T(8,128)(2,1)} %all-gather.2.cloned.1.call-done), kind=kOutput, calls=%fused_computation.10 | convolution fusion | flops 2149580800 | bytes 7340032 | tf_op jit(solution)/shard_map/dot_general | solution.py:55
  229.6 3.7 multiply_convert_fusion
  233.3 0.2 all-reduce.5.cloned.1.call-start
  233.5 5.5 %fusion.11 = bf16[1024,512]{1,0:T(8,128)(2,1)} fusion(bf16[512,2048]{1,0:T(8,128)(2,1)S(1)} %copy-done, bf16[1024,4096]{1,0:T(8,128)(2,1)} %all-gather.2.cloned.1.call-done), kind=kOutput, calls=%fused_computation.18 | convolution fusion | flops 2148007936 | bytes 7340032 | tf_op jit(solution)/shard_map/dot_general | solution.py:50
  239.1 0.2 convert_reduce_fusion.1
  239.3 2.8 convert_reduce_fusion
  242.1 8.4 %all-reduce = (bf16[2048]{0:T(1024)(128)(2,1)}, bf16[512]{0:T(512)(128)(2,1)}) all-reduce(bf16[2048]{0:T(1024)(128)(2,1)S(1)} %multiply_convert_fusion.2, bf16[512]{0:T(512)(128)(2,1)S(1)} %multiply_convert_fusion.3), channel_id=1, replica_groups=mesh['row'=8,'col'=8,'dp'=4] {'dp'}, use_global_device_ids=true, to_apply=%region_5.0 | all-reduce | flops 2560 | bytes 10240 | tf_op jit(solution)/shard_map/psum | solution.py:70
  250.5 83.4 %all-reduce.7.cloned.1.call-done = (bf16[512,2048]{0,1:T(8,128)(2,1)}, bf16[2048,512]{1,0:T(8,128)(2,1)}) async-done(((bf16[512,2048]{0,1:T(8,128)(2,1)}, bf16[2048,512]{1,0:T(8,128)(2,1)}), (bf16[512,2048]{0,1:T(8,128)(2,1)}, bf16[2048,512]{1,0:T(8,128)(2,1)})) %all-reduce.7.cloned.1.call-update) | async-done | bytes 4194320 | tf_op jit(solution)/shard_map/psum | solution.py:69
  333.9 3.9 copy.10
  337.8 82.7 %all-reduce.5.cloned.1.call-done = bf16[1024,512]{1,0:T(8,128)(2,1)} async-done(((bf16[1024,512]{1,0:T(8,128)(2,1)}), bf16[1024,512]{1,0:T(8,128)(2,1)}) %all-reduce.5.cloned.1.call-update) | async-done | bytes 1048592 | tf_op jit(solution)/shard_map/psum | solution.py:53
  420.5 2.3 copy.14
  422.8 3.0 copy.15
  (16 shorter events, 0.1 us)
Async XLA Ops:
  7.2 6.5 %copy-start = (bf16[512,2048]{1,0:T(8,128)(2,1)S(1)}, bf16[512,2048]{1,0:T(8,128)(2,1)}, u32[]{:S(2)}) copy-start(bf16[512,2048]{1,0:T(8,128)(2,1)} %param.7) | copy-start | bytes 6291460
  7.2 66.1 %reduce-scatter.5.cloned.1.call-start = ((), (), s32[]{:S(2)}) async-start(), calls=%async_computation.3 | async-start | bytes 4718592 | tf_op jit(solution)/shard_map/reduce_scatter | solution.py:41
  13.6 1.2 copy-start.4
  13.6 120.8 %reduce-scatter.3.cloned.1.call-start = ((), (), s32[]{:S(2)}) async-start(), calls=%async_computation.2 | async-start | bytes 4718592 | tf_op jit(solution)/shard_map/reduce_scatter | solution.py:34
  19.1 115.3 %copy-start.3 = (f32[2048]{0:T(1024)S(1)}, f32[2048]{0:T(1024)}, u32[]{:S(2)}) copy-start(f32[2048]{0:T(1024)} %param.8) | copy-start | bytes 24580
  19.1 204.1 %all-gather.2.cloned.1.call-start = ((), (), s32[]{:S(2)}) async-start(), calls=%async_computation.4 | async-start | bytes 9437184 | tf_op jit(solution)/shard_map/all_gather | solution.py:10
  137.6 92.0 %copy-start.2 = (bf16[1024,512]{1,0:T(8,128)(2,1)S(1)}, bf16[1024,512]{1,0:T(8,128)(2,1)}, u32[]{:S(2)}) copy-start(bf16[1024,512]{1,0:T(8,128)(2,1)} %param.6) | copy-start | bytes 3145732
  137.6 196.3 %all-reduce.7.cloned.1.call-start = ((), (), s32[]{:S(2)}) async-start(), calls=%async_computation.6 | async-start | bytes 8388608 | tf_op jit(solution)/shard_map/psum | solution.py:69
  223.2 6.3 %copy-start.1 = (bf16[1024,4096]{1,0:T(8,128)(2,1)S(1)}, bf16[1024,4096]{1,0:T(8,128)(2,1)}, u32[]{:S(2)}) copy-start(bf16[1024,4096]{1,0:T(8,128)(2,1)} %all-gather.2.cloned.1.call-done) | copy-start | bytes 25165828
  233.3 187.2 %all-reduce.5.cloned.1.call-start = ((), (), s32[]{:S(2)}) async-start(), calls=%async_computation.5 | async-start | bytes 2097152 | tf_op jit(solution)/shard_map/psum | solution.py:53
Sparse Core Ops, SparseCore 0:
  13.7 59.5 reduce-scatter.4
  75.9 58.5 reduce-scatter.2
  137.7 85.4 all-gather.1
  233.4 100.4 all-reduce.6
  337.0 83.4 all-reduce.4
where the time goes:
time: 435 us; the launch traced here: 432 us
  waiting for transfers between devices  367 us (84%)
  matrix products  26.2 us (6%)
  between operations  13.8 us (3%)
  local copies, waits for them, and re-layouts  10.4 us (2%)
  blocking collectives  8.42 us (2%)
  other arithmetic  6.18 us (1%)
    all_gather x1, waiting for transfers between devices, side_by_side(): whole = lax.all_gather(both, axis, axis=dim, tiled=True)  85.6 us
    psum x1, waiting for transfers between devices, local(): lax.psum(expand_part.astype(jnp.bfloat16), 'dp').astype(jnp.float32)  83.4 us
    psum x1, waiting for transfers between devices, local(): grad_inputs = lax.psum(input_part.astype(jnp.bfloat16), 'col')  82.7 us
    reduce_scatter x1, waiting for transfers between devices, local(): lax.psum_scatter(jnp.dot(row_block, expand, preferred_element_type=jnp.fl...  61.1 us
    reduce_scatter x1, waiting for transfers between devices, local(): lax.psum_scatter(back_product(row_block, contract).astype(jnp.bfloat16),...  54.1 us
    unnamed x13, local copies, waits for them, and re-layouts  10.4 us
  transfers between devices with their start and end apart: 5, of which 5 were waited for; matrix products, arithmetic and copies ran while one was open for 4% of the time, Pallas kernels for 0%

commit v1 on v0

v1 whole, which is shorter than its diff:
```python
import functools

import jax
import jax.numpy as jnp
from jax import lax
from jax.experimental import pallas as pl
from jax.experimental.pallas import tpu as pltpu
from jax.sharding import PartitionSpec as P

BF = jnp.bfloat16
F32 = jnp.float32
MESH = pl.DeviceIdType.MESH
NN = (((1,), (0,)), ((), ()))
NT = (((1,), (1,)), ((), ()))
TN = (((0,), (0,)), ((), ()))


def dot(a, b, dims):
    return lax.dot_general(a, b, dims, preferred_element_type=F32)


class Net:
    def __init__(self, send_sem, recv_sem):
        self.send_sem, self.recv_sem = send_sem, recv_sem
        self.used, self.sent = 0, []

    def ids(self, count):
        first = self.used
        self.used += count
        return range(first, first + count)

    def send(self, k, src, dst, device):
        copy = pltpu.make_async_remote_copy(
            src, dst, self.send_sem.at[k], self.recv_sem.at[k], device_id=device, device_id_type=MESH
        )
        copy.start()
        self.sent.append(copy)

    def arrived(self, k, dst, device):
        pltpu.make_async_remote_copy(
            dst, dst, self.send_sem.at[k], self.recv_sem.at[k], device_id=device, device_id_type=MESH
        ).wait_recv()

    def drain(self):
        for copy in self.sent:
            copy.wait_send()


class Gather:
    def __init__(self, net, me, left, right, full, top, bottom):
        self.net, self.me, self.left, self.right = net, me, left, right
        self.full, self.top, self.bottom = full, top, bottom
        self.k = net.ids(4)

    def start(self):
        block = self.full(self.me)
        self.net.send(self.k[0], block, block, self.right)
        self.net.send(self.k[1], block, block, self.left)

    def forward(self):
        before, after = (self.me + 3) % 4, (self.me + 1) % 4
        self.net.arrived(self.k[0], self.full(before), self.left)
        self.net.send(self.k[2], self.top(before), self.top(before), self.right)
        self.net.arrived(self.k[1], self.full(after), self.right)
        self.net.send(self.k[3], self.bottom(after), self.bottom(after), self.left)

    def finish(self):
        across = (self.me + 2) % 4
        self.net.arrived(self.k[2], self.top(across), self.left)
        self.net.arrived(self.k[3], self.bottom(across), self.right)


class Exchange:
    def __init__(self, net, me, left, right, src, dst, relay, rows):
        self.net, self.me, self.left, self.right = net, me, left, right
        self.src, self.dst, self.relay, self.rows = src, dst, relay, rows
        self.k = net.ids(6)

    def start(self):
        me, half = self.me, self.rows // 2
        before, after, across = (me + 3) % 4, (me + 1) % 4, (me + 2) % 4
        self.net.send(self.k[2], self.src(across, 0, half), self.relay.at[0], self.right)
        self.net.send(self.k[3], self.src(across, half, half), self.relay.at[1], self.left)
        self.net.send(self.k[0], self.src(after, 0, self.rows), self.dst(me, 0, self.rows), self.right)
        self.net.send(self.k[1], self.src(before, 0, self.rows), self.dst(me, 0, self.rows), self.left)

    def forward(self):
        me, half = self.me, self.rows // 2
        before, after = (me + 3) % 4, (me + 1) % 4
        self.net.arrived(self.k[2], self.relay.at[0], self.left)
        self.net.send(self.k[4], self.relay.at[0], self.dst(before, 0, half), self.right)
        self.net.arrived(self.k[3], self.relay.at[1], self.right)
        self.net.send(self.k[5], self.relay.at[1], self.dst(after, half, half), self.left)

    def near(self):
        me = self.me
        self.net.arrived(self.k[0], self.dst((me + 3) % 4, 0, self.rows), self.left)
        self.net.arrived(self.k[1], self.dst((me + 1) % 4, 0, self.rows), self.right)

    def finish(self):
        half, across = self.rows // 2, (self.me + 2) % 4
        self.net.arrived(self.k[4], self.dst(across, 0, half), self.left)
        self.net.arrived(self.k[5], self.dst(across, half, half), self.right)


class Reduce:
    def __init__(self, net, me, left, right, part, inbox, add, total):
        self.net, self.me, self.left, self.right = net, me, left, right
        self.part, self.inbox, self.add, self.total = part, inbox, add, total
        self.k = net.ids(6)

    def far(self):
        across = (self.me + 2) % 4
        self.net.send(self.k[0], self.part(across, 0), self.inbox.at[0], self.right)
        self.net.send(self.k[1], self.part(across, 1), self.inbox.at[1], self.left)

    def near(self):
        before, after = (self.me + 3) % 4, (self.me + 1) % 4
        self.net.send(self.k[2], self.part(after, 1), self.inbox.at[2], self.right)
        self.net.send(self.k[3], self.part(before, 0), self.inbox.at[3], self.left)

    def join(self):
        before, after = (self.me + 3) % 4, (self.me + 1) % 4
        self.net.arrived(self.k[0], self.inbox.at[0], self.left)
        self.add(self.part(after, 0), self.inbox.at[0])
        self.net.send(self.k[4], self.part(after, 0), self.inbox.at[4], self.right)
        self.net.arrived(self.k[1], self.inbox.at[1], self.right)
        self.add(self.part(before, 1), self.inbox.at[1])
        self.net.send(self.k[5], self.part(before, 1), self.inbox.at[5], self.left)

    def finish(self):
        self.net.arrived(self.k[3], self.inbox.at[3], self.right)
        self.net.arrived(self.k[4], self.inbox.at[4], self.left)
        self.total(0, self.part(self.me, 0), self.inbox.at[3], self.inbox.at[4])
        self.net.arrived(self.k[2], self.inbox.at[2], self.left)
        self.net.arrived(self.k[5], self.inbox.at[5], self.right)
        self.total(1, self.part(self.me, 1), self.inbox.at[2], self.inbox.at[5])


def add_into(target, other):
    rows = 64
    lead = target.shape[0] if len(target.shape) == 3 else 1
    depth = target.shape[-2]

    def view(ref, i, r):
        where = pl.ds(pl.multiple_of(r * rows, rows), rows)
        return ref.at[i, where] if len(ref.shape) == 3 else ref.at[where]

    @pl.loop(0, lead * (depth // rows))
    def _(n):
        i, r = n // (depth // rows), n % (depth // rows)
        mine = view(target, i, r)
        mine[...] = (mine[...].astype(F32) + view(other, i, r)[...].astype(F32)).astype(BF)


def total_into(out, parts):
    rows = 64
    lead = out.shape[0] if len(out.shape) == 3 else 1
    depth = out.shape[-2]

    def view(ref, i, r):
        where = pl.ds(pl.multiple_of(r * rows, rows), rows)
        return ref.at[i, where] if len(ref.shape) == 3 else ref.at[where]

    @pl.loop(0, lead * (depth // rows))
    def _(n):
        i, r = n // (depth // rows), n % (depth // rows)
        acc = view(parts[0], i, r)[...].astype(F32)
        for other in parts[1:]:
            acc = acc + view(other, i, r)[...].astype(F32)
        view(out, i, r)[...] = acc.astype(BF)


def rows_at(start, size, unit):
    return pl.ds(pl.multiple_of(start, unit), size)


def kernel(
    x_ref, u_ref, e_ref, b_ref, c_ref,
    ox_ref, oe_ref, ob_ref, oc_ref, oo_ref,
    xg, ug, eg, cg, part, got, ah, relay_e, relay_c,
    ge, gc, gx, in_e, in_c, in_x, sum_e, sum_c, sum_x, relay_ge, relay_gc,
    pair_in, pair_sum, in_z, small, small_in,
    send_sem, recv_sem, local_sem, hid_send, hid_recv, act_send, act_recv,
):
    row, col, x = lax.axis_index("row"), lax.axis_index("col"), lax.axis_index("dp")
    zh, c = row // 2, row % 2
    y, zl = col // 2, col % 2
    factor = 1.0 / 64.0

    z_right, z_left = {"row": ((zh + 1) % 4) * 2 + c}, {"row": ((zh + 3) % 4) * 2 + c}
    z_across = {"row": ((zh + 2) % 4) * 2 + c}
    y_right, y_left = {"col": ((y + 1) % 4) * 2 + zl}, {"col": ((y + 3) % 4) * 2 + zl}
    x_right, x_left, x_across = {"dp": (x + 1) % 4}, {"dp": (x + 3) % 4}, {"dp": (x + 2) % 4}
    twin = {"row": zh * 2 + 1 - c}
    beside = {"col": y * 2 + 1 - zl}

    locals_ = [
        pltpu.make_async_copy(x_ref, xg.at[zh], local_sem.at[0]),
        pltpu.make_async_copy(u_ref, ug.at[zh], local_sem.at[1]),
        pltpu.make_async_copy(e_ref.at[:, rows_at(zh * 512, 512, 512)], eg.at[zh], local_sem.at[2]),
        pltpu.make_async_copy(c_ref.at[rows_at(zh * 512, 512, 512)], cg.at[zh], local_sem.at[3]),
    ]
    for copy in locals_:
        copy.start()

    barrier = pltpu.get_barrier_semaphore()
    peers = (z_right, z_left, z_across, y_right, y_left, x_right, x_left, x_across, twin, beside)
    for peer in peers:
        pl.semaphore_signal(barrier, inc=1, device_id=peer, device_id_type=MESH)
    pl.semaphore_wait(barrier, len(peers))

    net = Net(send_sem, recv_sem)

    def token_block(buf, d, size=256, first=0):
        return lambda j: buf.at[d, rows_at(j * 256 + first, size, 128)]

    def z_gather(buf):
        def at(size, first):
            return lambda j: buf.at[j, rows_at(y * 256 + first, size, 128)]
        return Gather(net, zh, z_left, z_right, at(256, 0), at(128, 0), at(128, 128))

    def y_gathers(buf):
        return [
            Gather(net, y, y_left, y_right, token_block(buf, (zh + d) % 4),
                   token_block(buf, (zh + d) % 4, 128), token_block(buf, (zh + d) % 4, 128, 128))
            for d in (1, 2, 3)
        ]

    def x_gathers(buf):
        def at(d, size, first):
            return lambda j: buf.at[(zh + d) % 4, rows_at(j * 128 + first, size, 64)]
        return [
            Gather(net, x, x_left, x_right, at(d, 128, 0), at(d, 64, 0), at(d, 64, 64))
            for d in (1, 2, 3)
        ]

    def weight_slot(buf):
        return lambda j, first, size: buf.at[j, rows_at(x * 128 + first, size, 64)]

    xz, uz = z_gather(xg), z_gather(ug)
    xy, uy = y_gathers(xg), y_gathers(ug)
    ez = Exchange(
        net, zh, z_left, z_right,
        lambda j, first, size: e_ref.at[rows_at(x * 128 + first, size, 64), rows_at(j * 512, 512, 512)],
        weight_slot(eg), relay_e, 128,
    )
    cz = Exchange(
        net, zh, z_left, z_right,
        lambda j, first, size: c_ref.at[rows_at(j * 512 + x * 128 + first, size, 64)],
        weight_slot(cg), relay_c, 128,
    )
    ex, cx = x_gathers(eg), x_gathers(cg)

    locals_[0].wait()
    xz.start()
    ez.start()
    locals_[1].wait()
    xz.forward()
    xy[0].start()
    xy[2].start()
    uz.start()
    ez.forward()
    ez.near()
    ex[0].start()
    ex[2].start()
    cz.start()
    xy[0].forward()
    xy[2].forward()
    xz.finish()
    xy[1].start()
    ez.finish()
    ex[1].start()
    uz.forward()
    uy[0].start()
    uy[2].start()
    ex[0].forward()
    ex[2].forward()
    cz.forward()
    cz.near()
    cx[0].start()
    cx[2].start()
    xy[1].forward()
    ex[1].forward()
    uz.finish()
    uy[1].start()
    cz.finish()
    cx[1].start()
    uy[0].forward()
    uy[2].forward()
    cx[0].forward()
    cx[2].forward()
    cx[1].forward()
    uy[1].forward()
    locals_[2].wait()
    locals_[3].wait()
    for group in (ex, xy, cx, uy):
        for gather in group:
            gather.finish()

    def hid_copy(k, slot):
        return pltpu.make_async_remote_copy(
            part.at[k, slot, 1 - c], got.at[k, slot], hid_send.at[k, slot], hid_recv.at[k, slot],
            device_id=twin, device_id_type=MESH,
        )

    def act_copy(k, slot):
        block = ah.at[k, c, rows_at(slot * 256, 256, 256)]
        return pltpu.make_async_remote_copy(
            block, block, act_send.at[k, slot], act_recv.at[k, slot],
            device_id=twin, device_id_type=MESH,
        )

    def act_landing(k, slot):
        block = ah.at[k, 1 - c, rows_at(slot * 256, 256, 256)]
        return pltpu.make_async_remote_copy(
            block, block, act_send.at[k, slot], act_recv.at[k, slot],
            device_id=twin, device_id_type=MESH,
        )

    @pl.loop(0, 4)
    def _(slot):
        where = rows_at(slot * 256, 256, 256)
        for half in range(2):
            cols = pl.ds(half * 256, 256)
            acc = dot(xg[0, where], eg[0, :, cols], NN)
            for j in range(1, 4):
                acc = acc + dot(xg[j, where], eg[j, :, cols], NN)
            part[0, slot, half] = acc
            acc = dot(ug[0, where], cg[0, cols], NT)
            for j in range(1, 4):
                acc = acc + dot(ug[j, where], cg[j, cols], NT)
            part[1, slot, half] = acc
        hid_copy(0, slot).start()
        hid_copy(1, slot).start()

    @pl.loop(0, 4)
    def _(slot):
        hid_copy(0, slot).wait_recv()
        hid_copy(1, slot).wait_recv()
        bias = b_ref[row]

        @pl.loop(0, 8)
        def _(r):
            rows = rows_at(r * 32, 32, 32)
            pre = part[0, slot, c, rows] + got[0, slot, rows] + bias
            v = pre.astype(BF).astype(F32)
            back = (part[1, slot, c, rows] + got[1, slot, rows]).astype(BF).astype(F32)
            k0, k1 = 0.7978845608028654, 0.044715
            sq = v * v
            t = jnp.tanh(k0 * (v + k1 * (sq * v)))
            half = 0.5 * (1.0 + t)
            slope = half + (0.5 * v) * (1.0 - t * t) * (k0 * (1.0 + 3.0 * k1 * sq))
            out = rows_at(slot * 256 + r * 32, 32, 32)
            ah[0, c, out] = (v * half).astype(BF)
            ah[1, c, out] = (back * slope).astype(BF)

        act_copy(0, slot).start()
        act_copy(1, slot).start()

    @pl.loop(0, 4)
    def _(slot):
        for k in range(2):
            act_landing(k, slot).wait_recv()
            hid_copy(k, slot).wait_send()
            act_copy(k, slot).wait_send()

    e_red = Reduce(
        net, x, x_left, x_right, lambda j, h: ge.at[j, pl.ds(2 * h, 2)], in_e, add_into,
        lambda h, *parts: total_into(sum_e.at[pl.ds(2 * h, 2)], parts),
    )
    c_red = Reduce(
        net, x, x_left, x_right, lambda j, h: gc.at[j, pl.ds(2 * h, 2)], in_c, add_into,
        lambda h, *parts: total_into(sum_c.at[pl.ds(2 * h, 2)], parts),
    )
    x_red = Reduce(
        net, y, y_left, y_right, lambda j, h: gx.at[j, pl.ds(2 * h, 2)], in_x, add_into,
        lambda h, *parts: total_into(sum_x.at[pl.ds(2 * h, 2)], parts),
    )
    own_rows = ox_ref.at[col]
    z_red = Reduce(
        net, zh, z_left, z_right, lambda j, h: pair_sum.at[j, pl.ds(64 * h, 64)], in_z, add_into,
        lambda h, *parts: total_into(own_rows.at[pl.ds(64 * h, 64)], parts),
    )
    e_swap = Exchange(
        net, zh, z_left, z_right, lambda j, first, size: sum_e.at[j, pl.ds(first, size)],
        lambda j, first, size: oe_ref.at[x, j, pl.ds(first, size)], relay_ge, 128,
    )
    c_swap = Exchange(
        net, zh, z_left, z_right, lambda j, first, size: sum_c.at[j, pl.ds(first, size)],
        lambda j, first, size: oc_ref.at[x, j, pl.ds(first, size)], relay_gc, 128,
    )

    def out_gather(ref):
        return Gather(
            net, x, x_left, x_right, lambda j: ref.at[j],
            lambda j: ref.at[j, pl.ds(0, 2)], lambda j: ref.at[j, pl.ds(2, 2)],
        )

    e_out, c_out = out_gather(oe_ref), out_gather(oc_ref)
    x_out = Gather(
        net, y, y_left, y_right, lambda j: ox_ref.at[pl.ds(2 * j, 2)],
        lambda j: ox_ref.at[2 * j], lambda j: ox_ref.at[2 * j + 1],
    )

    @pl.loop(0, 4)
    def _(j):
        for h in range(2):
            acc = (dot(xg[j], ah[1, h], TN) * factor).astype(BF)
            for q in range(4):
                ge[q, j, :, pl.ds(h * 256, 256)] = acc[q * 128:(q + 1) * 128]

    e_red.far()
    e_red.near()

    @pl.loop(0, 4)
    def _(j):
        for h in range(2):
            acc = (dot(ah[0, h], ug[j], TN) * factor).astype(BF)
            gc[2 * h, j] = acc[:128]
            gc[2 * h + 1, j] = acc[128:]

    c_red.far()

    @pl.loop(0, 4)
    def _(slot):
        where = rows_at(slot * 256, 256, 256)
        for j in range(4):
            acc = dot(ah[1, 0, where], eg[j, :, pl.ds(0, 256)], NT)
            acc = acc + dot(ah[1, 1, where], eg[j, :, pl.ds(256, 256)], NT)
            gx[slot, j] = acc.astype(BF)

    x_red.far()
    x_red.near()
    e_red.join()
    c_red.near()

    for h in range(2):
        def add_rows(n, acc):
            block = ah[1, h, rows_at(n * 64, 64, 64)].astype(F32)
            return acc + jnp.sum(block.reshape(8, 8, 256), axis=0)
        acc = lax.fori_loop(0, 16, add_rows, jnp.zeros((8, 256), F32))
        acc = jnp.sum(acc, axis=0, keepdims=True) * factor
        small[pl.ds(0, 8), pl.ds(h * 256, 256)] = jnp.broadcast_to(acc.astype(BF).astype(F32), (8, 256))

    def add_up(n, acc):
        block = ug[zh, rows_at(n * 64, 64, 64)].astype(F32)
        return acc + jnp.sum(block.reshape(8, 8, 512), axis=0)
    acc = lax.fori_loop(0, 16, add_up, jnp.zeros((8, 512), F32))
    acc = jnp.sum(acc, axis=0, keepdims=True) * factor
    small[pl.ds(8, 8)] = jnp.broadcast_to(acc.astype(BF).astype(F32), (8, 512))
    small_k = net.ids(6)
    for n, peer in enumerate((x_right, x_left, x_across)):
        net.send(small_k[n], small, small_in.at[n], peer)

    c_red.join()
    x_red.join()
    for n, peer in enumerate((x_left, x_right, x_across)):
        net.arrived(small_k[n], small_in.at[n], peer)
    whole = ((small[...] + small_in[0]) + small_in[1]) + small_in[2]
    ob_ref[zh] = whole[:8]
    oo_ref[...] = whole[8:]
    for n, peer in enumerate((z_right, z_left, z_across)):
        net.send(small_k[3 + n], ob_ref.at[zh], ob_ref.at[zh], peer)

    e_red.finish()
    oe_ref[x, zh] = sum_e[zh]
    e_swap.start()
    c_red.finish()
    oc_ref[x, zh] = sum_c[zh]
    e_swap.forward()
    c_swap.start()
    e_swap.near()
    e_swap.finish()
    e_out.start()
    x_red.finish()
    pair_k = net.ids(2)
    net.send(pair_k[0], sum_x.at[:, rows_at((1 - zl) * 128, 128, 128)], pair_in, beside)
    c_swap.forward()
    c_swap.near()
    c_swap.finish()
    c_out.start()
    net.arrived(pair_k[0], pair_in, beside)

    @pl.loop(0, 4)
    def _(j):
        mine = sum_x[j, rows_at(zl * 128, 128, 128)].astype(F32)
        pair_sum[j] = (mine + pair_in[j].astype(F32)).astype(BF)

    z_red.far()
    z_red.near()
    z_red.join()
    e_out.forward()
    z_red.finish()
    net.send(pair_k[1], own_rows, own_rows, beside)
    net.arrived(pair_k[1], ox_ref.at[y * 2 + 1 - zl], beside)
    x_out.start()
    c_out.forward()
    x_out.forward()
    e_out.finish()
    x_out.finish()
    c_out.finish()
    for n, d in enumerate((3, 1, 2)):
        net.arrived(small_k[3 + n], ob_ref.at[(zh + d) % 4], z_across)
    net.drain()
    assert net.used <= 160


def local(inputs, upstream, expand, biases, contract):
    vmem = pl.BlockSpec(memory_space=pltpu.VMEM)
    anywhere = pl.BlockSpec(memory_space=pl.ANY)
    dma = pltpu.SemaphoreType.DMA
    ox, oe, ob, oc, oo = pl.pallas_call(
        kernel,
        out_shape=(
            jax.ShapeDtypeStruct((8, 128, 512), BF),
            jax.ShapeDtypeStruct((4, 4, 128, 512), BF),
            jax.ShapeDtypeStruct((4, 8, 512), F32),
            jax.ShapeDtypeStruct((4, 4, 128, 512), BF),
            jax.ShapeDtypeStruct((8, 512), F32),
        ),
        in_specs=[anywhere, anywhere, anywhere, vmem, anywhere],
        out_specs=(vmem, vmem, vmem, vmem, vmem),
        scratch_shapes=[
            pltpu.VMEM((4, 1024, 512), BF),
            pltpu.VMEM((4, 1024, 512), BF),
            pltpu.VMEM((4, 512, 512), BF),
            pltpu.VMEM((4, 512, 512), BF),
            pltpu.VMEM((2, 4, 2, 256, 256), F32),
            pltpu.VMEM((2, 4, 256, 256), F32),
            pltpu.VMEM((2, 2, 1024, 256), BF),
            pltpu.VMEM((2, 64, 512), BF),
            pltpu.VMEM((2, 64, 512), BF),
            pltpu.VMEM((4, 4, 128, 512), BF),
            pltpu.VMEM((4, 4, 128, 512), BF),
            pltpu.VMEM((4, 4, 256, 512), BF),
            pltpu.VMEM((6, 2, 128, 512), BF),
            pltpu.VMEM((6, 2, 128, 512), BF),
            pltpu.VMEM((6, 2, 256, 512), BF),
            pltpu.VMEM((4, 128, 512), BF),
            pltpu.VMEM((4, 128, 512), BF),
            pltpu.VMEM((4, 256, 512), BF),
            pltpu.VMEM((2, 64, 512), BF),
            pltpu.VMEM((2, 64, 512), BF),
            pltpu.VMEM((4, 128, 512), BF),
            pltpu.VMEM((4, 128, 512), BF),
            pltpu.VMEM((6, 64, 512), BF),
            pltpu.VMEM((16, 512), F32),
            pltpu.VMEM((3, 16, 512), F32),
            dma((160,)),
            dma((160,)),
            dma((4,)),
            dma((2, 4)),
            dma((2, 4)),
            dma((2, 4)),
            dma((2, 4)),
        ],
        compiler_params=pltpu.CompilerParams(
            collective_id=0, has_side_effects=True, vmem_limit_bytes=60 * 1024 * 1024
        ),
    )(inputs, upstream, expand, biases.reshape(8, 1, 256), contract)
    return (
        ox.reshape(1024, 512),
        oe.transpose(0, 2, 1, 3).reshape(512, 2048),
        ob[:, 0, :].reshape(2048).astype(BF),
        oc.transpose(1, 0, 2, 3).reshape(2048, 512),
        oo[0].astype(BF),
    )


def solution(mesh):
    in_specs = (P("dp", "row"), P("dp", "row"), P("row", "col"), P("col"), P("col", "row"))
    out_specs = (P("dp", "row"), P("row", "col"), P("col"), P("col", "row"), P("row"))
    return jax.shard_map(local, mesh=mesh, in_specs=in_specs, out_specs=out_specs, check_vma=False)
```

time: 435 us -> 212 us (0.49)
  waiting for transfers between devices: 367 us -> 0 us
  Pallas kernels: 0 us -> 200 us
  matrix products: 26.2 us -> 0 us
  between operations: 13.8 us -> 0.66 us
  blocking collectives: 8.42 us -> 0 us
  other arithmetic: 6.18 us -> 0 us
    pallas_call x0 -> x1, Pallas kernels: none -> 200 us  [local(): pl.pallas_call(kernel, out_shape=(jax.ShapeDtypeStruct((8, 128, 512), BF)...]
    psum x2 -> x0, waiting for transfers between devices: 166 us -> none  [the longest x1 83.4 us: local(): lax.psum(expand_part.astype(jnp.bfloat16), 'dp').astype(jnp.float32)]
    reduce_scatter x2 -> x0, waiting for transfers between devices: 115 us -> none  [the longest x1 61.1 us: local(): lax.psum_scatter(jnp.dot(row_block, expand, preferred_element_type=jnp.fl...]
    all_gather x1 -> x0, waiting for transfers between devices: 85.6 us -> none  [side_by_side(): whole = lax.all_gather(both, axis, axis=dim, tiled=True)]
    dot_general x5 -> x0, matrix products: 26.2 us -> none  [the longest x1 6.36 us: back_product(): lax.dot_general(upstream_rows, contract, (((1,), (1,)), ((), ())), prefer...]
    psum x1 -> x0, blocking collectives: 8.42 us -> none  [local(): lax.psum(biases_part.astype(jnp.bfloat16), 'dp').astype(jnp.float32)]
    unnamed x13 -> x7, local copies, waits for them, and re-layouts: 10.4 us -> 3.53 us
    transpose x0 -> x2, local copies, waits for them, and re-layouts: none -> 4.74 us  [the longest x1 3.21 us: local(): oe.transpose(0, 2, 1, 3).reshape(512, 2048)]
  transfers between devices with their start and end apart: 5 -> 0, of which waited for: 5 -> 0; matrix products, arithmetic and copies ran while one was open for 4% -> 0% of each run, Pallas kernels for 0% -> 0%
where the time goes in v1:
time: 212 us; the launch traced here: 211 us
  Pallas kernels  200 us (94%)
  local copies, waits for them, and re-layouts  10.4 us (5%)
    pallas_call x1, Pallas kernels, local(): pl.pallas_call(kernel, out_shape=(jax.ShapeDtypeStruct((8, 128, 512), BF)...  200 us

profile of v1, /device:TPU:8, one launch (start us, length us, event | category | flops | bytes accessed | tf_op | source)
XLA Modules:
  0.0 211.3 jit_solution(6324738028428725031)
XLA Ops:
  0.6 200.3 %shard_map.92 = (bf16[8,128,512]{2,1,0:T(8,128)(2,1)}, bf16[4,4,128,512]{3,2,1,0:T(8,128)(2,1)}, f32[4,8,512]{2,1,0:T(8,128)}, bf16[4,4,128,512]{3,2,1,0:T(8,128)(2,1)}, f32[8,512]{1,0:T(8,128)}) custom-call(bf16[1024,512]{1,0:T(8,128)(2,1)} %x_ref.1, bf16[1024,512]{1,0:T(8,128)(2,1)} %u_ref.1, bf16[512,2048]{1,0:T(8,128)(2,1)} %e_ref.1, ...), custom_call_target="tpu_custom_call" | custom-call | tf_op jit(solution)/shard_map/pallas_call | solution.py:513
  200.9 3.2 %copy.10 = bf16[4,128,4,512]{3,2,1,0:T(4,128)(2,1)S(1)} copy(bf16[4,128,4,512]{3,1,2,0:T(8,128)(2,1)} %bitcast.14) | data formatting | bytes 4194304 | tf_op jit(solution)/shard_map/transpose | solution.py:564
  204.1 0.0 copy-start
  204.1 2.0 copy.12
  206.1 1.3 fusion.1
  207.4 0.9 fusion
  208.2 0.6 copy.13
  208.8 0.0 copy-done
  208.8 0.0 copy-start.1
  208.8 1.5 copy.11
  210.4 0.0 copy-done.1
  210.4 1.0 copy.15
Async XLA Ops:
  204.1 4.7 %copy-start = (bf16[4,4,128,512]{3,2,1,0:T(8,128)(2,1)S(1)}, bf16[4,4,128,512]{3,2,1,0:T(8,128)(2,1)}, u32[]{:S(2)}) copy-start(bf16[4,4,128,512]{3,2,1,0:T(8,128)(2,1)} %get-tuple-element.13) | copy-start | bytes 6291460
  208.8 1.5 copy-start.1

commit v2 on v1

--- a/solution.py
+++ b/solution.py
@@ -138,7 +138,7 @@
 
 
 def add_into(target, other):
-    rows = 64
+    rows = min(64, target.shape[-2])
     lead = target.shape[0] if len(target.shape) == 3 else 1
     depth = target.shape[-2]
 
@@ -154,7 +154,7 @@
 
 
 def total_into(out, parts):
-    rows = 64
+    rows = min(64, out.shape[-2])
     lead = out.shape[0] if len(out.shape) == 3 else 1
     depth = out.shape[-2]
 
@@ -173,6 +173,38 @@
 
 def rows_at(start, size, unit):
     return pl.ds(pl.multiple_of(start, unit), size)
+
+
+class PairRing:
+    def __init__(self, net, zh, zl, outer, inner, block):
+        self.net, self.outer, self.inner, self.block = net, outer, inner, block
+        self.own, self.across = zh, (zh + 2) % 4
+        self.early, self.late = (zh + 3 + 2 * zl) % 4, (zh + 5 - 2 * zl) % 4
+        self.out_half, self.in_half = (1 - zl) * 128, zl * 128
+        self.k = net.ids(4)
+
+    def send(self, k, block, device):
+        self.net.send(self.k[k], block, block, device)
+
+    def start(self):
+        self.send(0, self.block(self.own, 0, 256), self.outer)
+
+    def get_early(self):
+        block = self.block(self.early, 0, 256)
+        self.net.arrived(self.k[0], block, self.outer)
+        self.send(1, block, self.inner)
+
+    def get_late(self):
+        self.net.arrived(self.k[1], self.block(self.late, 0, 256), self.inner)
+        self.send(2, self.block(self.late, self.out_half, 128), self.outer)
+
+    def get_across(self):
+        block = self.block(self.across, self.in_half, 128)
+        self.net.arrived(self.k[2], block, self.outer)
+        self.send(3, block, self.inner)
+
+    def finish(self):
+        self.net.arrived(self.k[3], self.block(self.across, self.out_half, 128), self.inner)
 
 
 def kernel(
@@ -194,6 +226,7 @@
     x_right, x_left, x_across = {"dp": (x + 1) % 4}, {"dp": (x + 3) % 4}, {"dp": (x + 2) % 4}
     twin = {"row": zh * 2 + 1 - c}
     beside = {"col": y * 2 + 1 - zl}
+    outer = {"row": ((zh + 3 + 2 * zl) % 4) * 2 + c, "col": y * 2 + 1 - zl}
 
     locals_ = [
         pltpu.make_async_copy(x_ref, xg.at[zh], local_sem.at[0]),
@@ -205,41 +238,40 @@
         copy.start()
 
     barrier = pltpu.get_barrier_semaphore()
-    peers = (z_right, z_left, z_across, y_right, y_left, x_right, x_left, x_across, twin, beside)
+    peers = (z_right, z_left, z_across, y_right, y_left, x_right, x_left, x_across, twin, beside, outer)
     for peer in peers:
         pl.semaphore_signal(barrier, inc=1, device_id=peer, device_id_type=MESH)
     pl.semaphore_wait(barrier, len(peers))
 
     net = Net(send_sem, recv_sem)
 
-    def token_block(buf, d, size=256, first=0):
-        return lambda j: buf.at[d, rows_at(j * 256 + first, size, 128)]
-
     def z_gather(buf):
-        def at(size, first):
-            return lambda j: buf.at[j, rows_at(y * 256 + first, size, 128)]
-        return Gather(net, zh, z_left, z_right, at(256, 0), at(128, 0), at(128, 128))
-
-    def y_gathers(buf):
+        return PairRing(
+            net, zh, zl, outer, beside, lambda j, first, size: buf.at[j, rows_at(y * 256 + first, size, 128)]
+        )
+
+    def y_gathers(buf, ring):
+        def gather(d):
+            def at(size, first):
+                return lambda j: buf.at[d, rows_at(j * 256 + first, size, 128)]
+            return Gather(net, y, y_left, y_right, at(256, 0), at(128, 0), at(128, 128))
+        return [gather(d) for d in (ring.early, ring.late, ring.across)]
+
+    def x_gathers(at, order):
         return [
-            Gather(net, y, y_left, y_right, token_block(buf, (zh + d) % 4),
-                   token_block(buf, (zh + d) % 4, 128), token_block(buf, (zh + d) % 4, 128, 128))
-            for d in (1, 2, 3)
+            Gather(net, x, x_left, x_right, at(d, 128, 0), at(d, 64, 0), at(d, 64, 64)) for d in order
         ]
 
-    def x_gathers(buf):
-        def at(d, size, first):
-            return lambda j: buf.at[(zh + d) % 4, rows_at(j * 128 + first, size, 64)]
-        return [
-            Gather(net, x, x_left, x_right, at(d, 128, 0), at(d, 64, 0), at(d, 64, 64))
-            for d in (1, 2, 3)
-        ]
+    others = [(zh + d) % 4 for d in (3, 1, 2)]
+
+    def weight_at(buf):
+        return lambda d, size, first: lambda j: buf.at[d, rows_at(j * 128 + first, size, 64)]
 
     def weight_slot(buf):
         return lambda j, first, size: buf.at[j, rows_at(x * 128 + first, size, 64)]
 
     xz, uz = z_gather(xg), z_gather(ug)
-    xy, uy = y_gathers(xg), y_gathers(ug)
+    xy, uy = y_gathers(xg, xz), y_gathers(ug, uz)
     ez = Exchange(
         net, zh, z_left, z_right,
         lambda j, first, size: e_ref.at[rows_at(x * 128 + first, size, 64), rows_at(j * 512, 512, 512)],
@@ -250,53 +282,7 @@
         lambda j, first, size: c_ref.at[rows_at(j * 512 + x * 128 + first, size, 64)],
         weight_slot(cg), relay_c, 128,
     )
-    ex, cx = x_gathers(eg), x_gathers(cg)
-
-    locals_[0].wait()
-    xz.start()
-    ez.start()
-    locals_[1].wait()
-    xz.forward()
-    xy[0].start()
-    xy[2].start()
-    uz.start()
-    ez.forward()
-    ez.near()
-    ex[0].start()
-    ex[2].start()
-    cz.start()
-    xy[0].forward()
-    xy[2].forward()
-    xz.finish()
-    xy[1].start()
-    ez.finish()
-    ex[1].start()
-    uz.forward()
-    uy[0].start()
-    uy[2].start()
-    ex[0].forward()
-    ex[2].forward()
-    cz.forward()
-    cz.near()
-    cx[0].start()
-    cx[2].start()
-    xy[1].forward()
-    ex[1].forward()
-    uz.finish()
-    uy[1].start()
-    cz.finish()
-    cx[1].start()
-    uy[0].forward()
-    uy[2].forward()
-    cx[0].forward()
-    cx[2].forward()
-    cx[1].forward()
-    uy[1].forward()
-    locals_[2].wait()
-    locals_[3].wait()
-    for group in (ex, xy, cx, uy):
-        for gather in group:
-            gather.finish()
+    ex, cx = x_gathers(weight_at(eg), others), x_gathers(weight_at(cg), others)
 
     def hid_copy(k, slot):
         return pltpu.make_async_remote_copy(
@@ -304,25 +290,19 @@
             device_id=twin, device_id_type=MESH,
         )
 
-    def act_copy(k, slot):
-        block = ah.at[k, c, rows_at(slot * 256, 256, 256)]
+    def act_copy(k, slot, half):
+        block = ah.at[k, half, rows_at(slot * 256, 256, 256)]
         return pltpu.make_async_remote_copy(
             block, block, act_send.at[k, slot], act_recv.at[k, slot],
             device_id=twin, device_id_type=MESH,
         )
 
-    def act_landing(k, slot):
-        block = ah.at[k, 1 - c, rows_at(slot * 256, 256, 256)]
-        return pltpu.make_async_remote_copy(
-            block, block, act_send.at[k, slot], act_recv.at[k, slot],
-            device_id=twin, device_id_type=MESH,
-        )
-
-    @pl.loop(0, 4)
-    def _(slot):
+    def partials(slot):
         where = rows_at(slot * 256, 256, 256)
-        for half in range(2):
-            cols = pl.ds(half * 256, 256)
+
+        @pl.loop(0, 2)
+        def _(half):
+            cols = rows_at(half * 256, 256, 256)
             acc = dot(xg[0, where], eg[0, :, cols], NN)
             for j in range(1, 4):
                 acc = acc + dot(xg[j, where], eg[j, :, cols], NN)
@@ -331,11 +311,11 @@
             for j in range(1, 4):
                 acc = acc + dot(ug[j, where], cg[j, cols], NT)
             part[1, slot, half] = acc
+
         hid_copy(0, slot).start()
         hid_copy(1, slot).start()
 
-    @pl.loop(0, 4)
-    def _(slot):
+    def pointwise(slot):
         hid_copy(0, slot).wait_recv()
         hid_copy(1, slot).wait_recv()
         bias = b_ref[row]
@@ -355,53 +335,137 @@
             ah[0, c, out] = (v * half).astype(BF)
             ah[1, c, out] = (back * slope).astype(BF)
 
-        act_copy(0, slot).start()
-        act_copy(1, slot).start()
+        act_copy(0, slot, c).start()
+        act_copy(1, slot, c).start()
+
+    locals_[0].wait()
+    xz.start()
+    locals_[1].wait()
+    uz.start()
+    xz.get_early()
+    xy[0].start()
+    ez.start()
+    uz.get_early()
+    uy[0].start()
+    xz.get_late()
+    xy[1].start()
+    uz.get_late()
+    uy[1].start()
+    xy[0].forward()
+    xz.get_across()
+    ez.forward()
+    ez.near()
+    ex[0].start()
+    ex[1].start()
+    uy[0].forward()
+    uz.get_across()
+    xz.finish()
+    xy[2].start()
+    cz.start()
+    ez.finish()
+    ex[2].start()
+    xy[1].forward()
+    uz.finish()
+    uy[2].start()
+    ex[0].forward()
+    ex[1].forward()
+    uy[1].forward()
+    cz.forward()
+    cz.near()
+    cx[0].start()
+    cx[1].start()
+    cz.finish()
+    cx[2].start()
+    ex[2].forward()
+    xy[2].forward()
+    cx[0].forward()
+    cx[1].forward()
+    cx[2].forward()
+    locals_[2].wait()
+    locals_[3].wait()
+    for gather in ex + cx:
+        gather.finish()
+    partials(y)
+    uy[2].forward()
+
+    @pl.loop(0, 2)
+    def _(n):
+        partials((y + 1 + 2 * n) % 4)
+
+    pointwise(y)
+    for gather in xy + uy:
+        gather.finish()
+    partials((y + 2) % 4)
+
+    @pl.loop(0, 3)
+    def _(n):
+        pointwise((y + 1 + 2 * n - n // 2 * 3) % 4)
 
     @pl.loop(0, 4)
     def _(slot):
         for k in range(2):
-            act_landing(k, slot).wait_recv()
+            act_copy(k, slot, 1 - c).wait_recv()
             hid_copy(k, slot).wait_send()
-            act_copy(k, slot).wait_send()
-
-    e_red = Reduce(
-        net, x, x_left, x_right, lambda j, h: ge.at[j, pl.ds(2 * h, 2)], in_e, add_into,
-        lambda h, *parts: total_into(sum_e.at[pl.ds(2 * h, 2)], parts),
-    )
-    c_red = Reduce(
-        net, x, x_left, x_right, lambda j, h: gc.at[j, pl.ds(2 * h, 2)], in_c, add_into,
-        lambda h, *parts: total_into(sum_c.at[pl.ds(2 * h, 2)], parts),
-    )
-    x_red = Reduce(
-        net, y, y_left, y_right, lambda j, h: gx.at[j, pl.ds(2 * h, 2)], in_x, add_into,
-        lambda h, *parts: total_into(sum_x.at[pl.ds(2 * h, 2)], parts),
-    )
-    own_rows = ox_ref.at[col]
-    z_red = Reduce(
-        net, zh, z_left, z_right, lambda j, h: pair_sum.at[j, pl.ds(64 * h, 64)], in_z, add_into,
-        lambda h, *parts: total_into(own_rows.at[pl.ds(64 * h, 64)], parts),
-    )
-    e_swap = Exchange(
-        net, zh, z_left, z_right, lambda j, first, size: sum_e.at[j, pl.ds(first, size)],
-        lambda j, first, size: oe_ref.at[x, j, pl.ds(first, size)], relay_ge, 128,
-    )
-    c_swap = Exchange(
-        net, zh, z_left, z_right, lambda j, first, size: sum_c.at[j, pl.ds(first, size)],
-        lambda j, first, size: oc_ref.at[x, j, pl.ds(first, size)], relay_gc, 128,
-    )
-
-    def out_gather(ref):
-        return Gather(
-            net, x, x_left, x_right, lambda j: ref.at[j],
-            lambda j: ref.at[j, pl.ds(0, 2)], lambda j: ref.at[j, pl.ds(2, 2)],
-        )
-
-    e_out, c_out = out_gather(oe_ref), out_gather(oc_ref)
-    x_out = Gather(
-        net, y, y_left, y_right, lambda j: ox_ref.at[pl.ds(2 * j, 2)],
-        lambda j: ox_ref.at[2 * j], lambda j: ox_ref.at[2 * j + 1],
-    )
+            act_copy(k, slot, c).wait_send()
+
+    def reduce_to(axis, part_at, inbox, out):
+        me, left, right = axis
+        return Reduce(net, me, left, right, part_at, inbox, add_into,
+                      lambda h, *parts: total_into(out(h), parts))
+
+    over_x, over_y, over_z = (x, x_left, x_right), (y, y_left, y_right), (zh, z_left, z_right)
+    e_red = reduce_to(over_x, lambda j, h: ge.at[j, pl.ds(2 * h, 2)], in_e, lambda h: sum_e.at[pl.ds(2 * h, 2)])
+    c_red = reduce_to(over_x, lambda j, h: gc.at[j, pl.ds(2 * h, 2)], in_c, lambda h: sum_c.at[pl.ds(2 * h, 2)])
+
+    def own_rows(s, first, size):
+        return ox_ref.at[rows_at(y * 256 + s * 128 + zl * 64 + first, size, 32)]
+
+    def per_chunk(s):
+        down = reduce_to(over_y, lambda j, h: gx.at[s, j, pl.ds(2 * h, 2)], in_x.at[s],
+                         lambda h: sum_x.at[s, pl.ds(2 * h, 2)])
+        along = reduce_to(over_z, lambda j, h: pair_sum.at[s, j, pl.ds(32 * h, 32)], in_z.at[s],
+                          lambda h: own_rows(s, 32 * h, 32))
+        def at(size, first):
+            return lambda j: ox_ref.at[rows_at(j * 256 + s * 128 + first, size, 64)]
+        spread = Gather(net, y, y_left, y_right, at(128, 0), at(64, 0), at(64, 64))
+        return down, along, spread, net.ids(2)
+
+    chunks = [per_chunk(s) for s in range(2)]
+
+    def out_e(j, first, size):
+        return oe_ref.at[rows_at(x * 128 + first, size, 64), rows_at(j * 512, 512, 512)]
+
+    def out_c(j, first, size):
+        return oc_ref.at[rows_at(j * 512 + x * 128 + first, size, 64)]
+
+    e_swap = Exchange(net, zh, z_left, z_right, lambda j, first, size: sum_e.at[j, pl.ds(first, size)],
+                      out_e, relay_ge, 128)
+    c_swap = Exchange(net, zh, z_left, z_right, lambda j, first, size: sum_c.at[j, pl.ds(first, size)],
+                      out_c, relay_gc, 128)
+    order = [zh] + others
+    e_out = x_gathers(
+        lambda d, size, first: lambda j: oe_ref.at[rows_at(j * 128 + first, size, 64), rows_at(d * 512, 512, 512)],
+        order)
+    c_out = x_gathers(
+        lambda d, size, first: lambda j: oc_ref.at[rows_at(d * 512 + j * 128 + first, size, 64)], order)
+
+    def pair_send(s):
+        net.send(chunks[s][3][0], sum_x.at[s, :, rows_at((1 - zl) * 64, 64, 64)], pair_in.at[s], beside)
+
+    def pair_add(s):
+        net.arrived(chunks[s][3][0], pair_in.at[s], beside)
+
+        @pl.loop(0, 4)
+        def _(j):
+            mine = sum_x[s, j, rows_at(zl * 64, 64, 64)].astype(F32)
+            pair_sum[s, j] = (mine + pair_in[s, j].astype(F32)).astype(BF)
+
+    def pair_back(s):
+        net.send(chunks[s][3][1], own_rows(s, 0, 64), own_rows(s, 0, 64), beside)
+
+    def pair_got(s):
+        there = ox_ref.at[rows_at(y * 256 + s * 128 + (1 - zl) * 64, 64, 64)]
+        net.arrived(chunks[s][3][1], there, beside)
 
     @pl.loop(0, 4)
     def _(j):
@@ -412,6 +476,18 @@
 
     e_red.far()
     e_red.near()
+    for s in range(2):
+        @pl.loop(0, 4)
+        def _(slot):
+            where = rows_at(slot * 256 + s * 128, 128, 128)
+            for j in range(4):
+                acc = dot(ah[1, 0, where], eg[j, :, pl.ds(0, 256)], NT)
+                acc = acc + dot(ah[1, 1, where], eg[j, :, pl.ds(256, 256)], NT)
+                gx[s, slot, j] = acc.astype(BF)
+        chunks[s][0].far()
+        if s == 0:
+            chunks[s][0].near()
+    e_red.join()
 
     @pl.loop(0, 4)
     def _(j):
@@ -421,19 +497,9 @@
             gc[2 * h + 1, j] = acc[128:]
 
     c_red.far()
-
-    @pl.loop(0, 4)
-    def _(slot):
-        where = rows_at(slot * 256, 256, 256)
-        for j in range(4):
-            acc = dot(ah[1, 0, where], eg[j, :, pl.ds(0, 256)], NT)
-            acc = acc + dot(ah[1, 1, where], eg[j, :, pl.ds(256, 256)], NT)
-            gx[slot, j] = acc.astype(BF)
-
-    x_red.far()
-    x_red.near()
-    e_red.join()
     c_red.near()
+    chunks[0][0].join()
+    chunks[1][0].near()
 
     for h in range(2):
         def add_rows(n, acc):
@@ -453,8 +519,15 @@
     for n, peer in enumerate((x_right, x_left, x_across)):
         net.send(small_k[n], small, small_in.at[n], peer)
 
+    e_red.finish()
+    e_swap.start()
+    oe_ref[rows_at(x * 128, 128, 128), rows_at(zh * 512, 512, 512)] = sum_e[zh]
+    e_out[0].start()
+    chunks[1][0].join()
     c_red.join()
-    x_red.join()
+    e_swap.forward()
+    chunks[0][0].finish()
+    pair_send(0)
     for n, peer in enumerate((x_left, x_right, x_across)):
         net.arrived(small_k[n], small_in.at[n], peer)
     whole = ((small[...] + small_in[0]) + small_in[1]) + small_in[2]
@@ -462,48 +535,74 @@
     oo_ref[...] = whole[8:]
     for n, peer in enumerate((z_right, z_left, z_across)):
         net.send(small_k[3 + n], ob_ref.at[zh], ob_ref.at[zh], peer)
-
-    e_red.finish()
-    oe_ref[x, zh] = sum_e[zh]
-    e_swap.start()
+    e_swap.near()
+    e_out[1].start()
+    e_out[2].start()
+    pair_add(0)
+    chunks[0][1].far()
+    chunks[0][1].near()
+    e_swap.finish()
+    e_out[3].start()
     c_red.finish()
-    oc_ref[x, zh] = sum_c[zh]
-    e_swap.forward()
     c_swap.start()
-    e_swap.near()
-    e_swap.finish()
-    e_out.start()
-    x_red.finish()
-    pair_k = net.ids(2)
-    net.send(pair_k[0], sum_x.at[:, rows_at((1 - zl) * 128, 128, 128)], pair_in, beside)
+    oc_ref[rows_at(zh * 512 + x * 128, 128, 128)] = sum_c[zh]
+    c_out[0].start()
+    chunks[1][0].finish()
+    pair_send(1)
+    chunks[0][1].join()
+    e_out[0].forward()
     c_swap.forward()
+    chunks[0][1].finish()
+    pair_back(0)
+    pair_add(1)
+    chunks[1][1].far()
+    chunks[1][1].near()
+    e_out[1].forward()
+    e_out[2].forward()
+    pair_got(0)
+    chunks[0][2].start()
     c_swap.near()
+    c_out[1].start()
+    c_out[2].start()
+    chunks[1][1].join()
+    e_out[3].forward()
     c_swap.finish()
-    c_out.start()
-    net.arrived(pair_k[0], pair_in, beside)
-
-    @pl.loop(0, 4)
-    def _(j):
-        mine = sum_x[j, rows_at(zl * 128, 128, 128)].astype(F32)
-        pair_sum[j] = (mine + pair_in[j].astype(F32)).astype(BF)
-
-    z_red.far()
-    z_red.near()
-    z_red.join()
-    e_out.forward()
-    z_red.finish()
-    net.send(pair_k[1], own_rows, own_rows, beside)
-    net.arrived(pair_k[1], ox_ref.at[y * 2 + 1 - zl], beside)
-    x_out.start()
-    c_out.forward()
-    x_out.forward()
-    e_out.finish()
-    x_out.finish()
-    c_out.finish()
+    c_out[3].start()
+    chunks[1][1].finish()
+    pair_back(1)
+    c_out[0].forward()
+    chunks[0][2].forward()
+    pair_got(1)
+    chunks[1][2].start()
+    c_out[1].forward()
+    c_out[2].forward()
+    chunks[1][2].forward()
+    c_out[3].forward()
+    for gather in e_out + c_out:
+        gather.finish()
+    for chunk in chunks:
+        chunk[2].finish()
     for n, d in enumerate((3, 1, 2)):
         net.arrived(small_k[3 + n], ob_ref.at[(zh + d) % 4], z_across)
     net.drain()
-    assert net.used <= 160
+    assert net.used <= 224
+
+
+def finish(ox, oe, ob, oc, oo, gx, ge, gb, gc, go, tall, wide, sem):
+    copies = [
+        pltpu.make_async_copy(src, dst, sem.at[k]) for k, (src, dst) in enumerate(((oe, ge), (oc, gc), (ox, gx)))
+    ]
+    for copy in copies:
+        copy.start()
+    for k in range(4):
+        cols = pl.ds(k * 128, 128)
+        for j in range(4):
+            tall[pl.ds(j * 4 + k, 1)] = ob[j, pl.ds(0, 1), cols]
+        wide[pl.ds(k, 1)] = oo[pl.ds(0, 1), cols]
+    gb[...] = tall[...].astype(BF)
+    go[...] = wide[...].astype(BF)
+    for copy in copies:
+        copy.wait()
 
 
 def local(inputs, upstream, expand, biases, contract):
@@ -513,11 +612,11 @@
     ox, oe, ob, oc, oo = pl.pallas_call(
         kernel,
         out_shape=(
-            jax.ShapeDtypeStruct((8, 128, 512), BF),
-            jax.ShapeDtypeStruct((4, 4, 128, 512), BF),
-            jax.ShapeDtypeStruct((4, 8, 512), F32),
-            jax.ShapeDtypeStruct((4, 4, 128, 512), BF),
-            jax.ShapeDtypeStruct((8, 512), F32),
+            pltpu.VMEM((1024, 512), BF),
+            pltpu.VMEM((512, 2048), BF),
+            pltpu.VMEM((4, 8, 512), F32),
+            pltpu.VMEM((2048, 512), BF),
+            pltpu.VMEM((8, 512), F32),
         ),
         in_specs=[anywhere, anywhere, anywhere, vmem, anywhere],
         out_specs=(vmem, vmem, vmem, vmem, vmem),
@@ -533,22 +632,22 @@
             pltpu.VMEM((2, 64, 512), BF),
             pltpu.VMEM((4, 4, 128, 512), BF),
             pltpu.VMEM((4, 4, 128, 512), BF),
-            pltpu.VMEM((4, 4, 256, 512), BF),
+            pltpu.VMEM((2, 4, 4, 128, 512), BF),
             pltpu.VMEM((6, 2, 128, 512), BF),
             pltpu.VMEM((6, 2, 128, 512), BF),
-            pltpu.VMEM((6, 2, 256, 512), BF),
+            pltpu.VMEM((2, 6, 2, 128, 512), BF),
             pltpu.VMEM((4, 128, 512), BF),
             pltpu.VMEM((4, 128, 512), BF),
-            pltpu.VMEM((4, 256, 512), BF),
+            pltpu.VMEM((2, 4, 128, 512), BF),
             pltpu.VMEM((2, 64, 512), BF),
             pltpu.VMEM((2, 64, 512), BF),
-            pltpu.VMEM((4, 128, 512), BF),
-            pltpu.VMEM((4, 128, 512), BF),
-            pltpu.VMEM((6, 64, 512), BF),
+            pltpu.VMEM((2, 4, 64, 512), BF),
+            pltpu.VMEM((2, 4, 64, 512), BF),
+            pltpu.VMEM((2, 6, 32, 512), BF),
             pltpu.VMEM((16, 512), F32),
             pltpu.VMEM((3, 16, 512), F32),
-            dma((160,)),
-            dma((160,)),
+            dma((224,)),
+            dma((224,)),
             dma((4,)),
             dma((2, 4)),
             dma((2, 4)),
@@ -556,16 +655,24 @@
             dma((2, 4)),
         ],
         compiler_params=pltpu.CompilerParams(
-            collective_id=0, has_side_effects=True, vmem_limit_bytes=60 * 1024 * 1024
+            collective_id=0, has_side_effects=True, vmem_limit_bytes=50 * 1024 * 1024
         ),
     )(inputs, upstream, expand, biases.reshape(8, 1, 256), contract)
-    return (
-        ox.reshape(1024, 512),
-        oe.transpose(0, 2, 1, 3).reshape(512, 2048),
-        ob[:, 0, :].reshape(2048).astype(BF),
-        oc.transpose(1, 0, 2, 3).reshape(2048, 512),
-        oo[0].astype(BF),
-    )
+    gx, ge, gb, gc, go = pl.pallas_call(
+        finish,
+        out_shape=(
+            jax.ShapeDtypeStruct((1024, 512), BF),
+            jax.ShapeDtypeStruct((512, 2048), BF),
+            jax.ShapeDtypeStruct((16, 128), BF),
+            jax.ShapeDtypeStruct((2048, 512), BF),
+            jax.ShapeDtypeStruct((4, 128), BF),
+        ),
+        in_specs=[vmem] * 5,
+        out_specs=(anywhere, anywhere, vmem, anywhere, vmem),
+        scratch_shapes=[pltpu.VMEM((16, 128), F32), pltpu.VMEM((4, 128), F32), dma((3,))],
+        compiler_params=pltpu.CompilerParams(vmem_limit_bytes=12 * 1024 * 1024),
+    )(ox, oe, ob, oc, oo)
+    return gx, ge, gb.reshape(2048), gc, go.reshape(512)
 
 
 def solution(mesh):

time: 212 us -> 176 us (0.83)
  Pallas kernels: 200 us -> 175 us
  local copies, waits for them, and re-layouts: 10.4 us -> 0 us
    pallas_call x1 -> x2, Pallas kernels: 200 us -> 175 us  [the longest x1 172 us: local(): pl.pallas_call(kernel, out_shape=(pltpu.VMEM((1024, 512), BF), pltpu.VMEM...]
    transpose x2 -> x0, local copies, waits for them, and re-layouts: 4.74 us -> none  [the longest x1 3.21 us: local(): oe.transpose(0, 2, 1, 3).reshape(512, 2048)]
    unnamed x7 -> x0, local copies, waits for them, and re-layouts: 3.53 us -> none
    slice x2 -> x0, local copies, waits for them, and re-layouts: 2.16 us -> none  [the longest x1 1.3 us: local(): oo[0].astype(BF)]
where the time goes in v2:
time: 176 us; the launch traced here: 175 us
  Pallas kernels  175 us (99%)
    pallas_call x1, Pallas kernels, local(): pl.pallas_call(kernel, out_shape=(pltpu.VMEM((1024, 512), BF), pltpu.VMEM...  172 us

profile of v2, /device:TPU:8, one launch (start us, length us, event | category | flops | bytes accessed | tf_op | source)
XLA Modules:
  0.0 175.5 jit_solution(5911739742562145319)
XLA Ops:
  0.6 171.9 %shard_map.92 = (bf16[1024,512]{1,0:T(8,128)(2,1)S(1)}, bf16[512,2048]{1,0:T(8,128)(2,1)S(1)}, f32[4,8,512]{2,1,0:T(8,128)S(1)}, bf16[2048,512]{1,0:T(8,128)(2,1)S(1)}, f32[8,512]{1,0:T(8,128)S(1)}) custom-call(bf16[1024,512]{1,0:T(8,128)(2,1)} %x_ref.1, bf16[1024,512]{1,0:T(8,128)(2,1)} %u_ref.1, bf16[512,2048]{1,0:T(8,128)(2,1)} %e_ref.1, ...), custom_call_target="tpu_custom_call" | custom-call | tf_op jit(solution)/shard_map/pallas_call | solution.py:612
  172.5 3.0 %shard_map.93 = (bf16[1024,512]{1,0:T(8,128)(2,1)}, bf16[512,2048]{1,0:T(8,128)(2,1)}, bf16[16,128]{1,0:T(8,128)(2,1)}, bf16[2048,512]{1,0:T(8,128)(2,1)}, bf16[4,128]{1,0:T(4,128)(2,1)}) custom-call(bf16[1024,512]{1,0:T(8,128)(2,1)S(1)} %get-tuple-element.15.ox, bf16[512,2048]{1,0:T(8,128)(2,1)S(1)} %get-tuple-element.16.oe, ...), custom_call_target="tpu_custom_call" | custom-call | tf_op jit(solution)/shard_map/pallas_call | solution.py:661

commit v3 on v2

--- a/solution.py
+++ b/solution.py
@@ -56,6 +56,10 @@
         block = self.full(self.me)
         self.net.send(self.k[0], block, block, self.right)
         self.net.send(self.k[1], block, block, self.left)
+
+    def near(self):
+        self.net.arrived(self.k[0], self.full((self.me + 3) % 4), self.left)
+        self.net.arrived(self.k[1], self.full((self.me + 1) % 4), self.right)
 
     def forward(self):
         before, after = (self.me + 3) % 4, (self.me + 1) % 4
@@ -245,9 +249,9 @@
 
     net = Net(send_sem, recv_sem)
 
-    def z_gather(buf):
+    def z_gather(buf, slot):
         return PairRing(
-            net, zh, zl, outer, beside, lambda j, first, size: buf.at[j, rows_at(y * 256 + first, size, 128)]
+            net, zh, zl, outer, beside, lambda j, first, size: buf.at[j, rows_at(slot * 256 + first, size, 128)]
         )
 
     def y_gathers(buf, ring):
@@ -270,7 +274,7 @@
     def weight_slot(buf):
         return lambda j, first, size: buf.at[j, rows_at(x * 128 + first, size, 64)]
 
-    xz, uz = z_gather(xg), z_gather(ug)
+    xz, uz = z_gather(xg, y), z_gather(ug, y)
     xy, uy = y_gathers(xg, xz), y_gathers(ug, uz)
     ez = Exchange(
         net, zh, z_left, z_right,
@@ -338,75 +342,13 @@
         act_copy(0, slot, c).start()
         act_copy(1, slot, c).start()
 
-    locals_[0].wait()
-    xz.start()
-    locals_[1].wait()
-    uz.start()
-    xz.get_early()
-    xy[0].start()
-    ez.start()
-    uz.get_early()
-    uy[0].start()
-    xz.get_late()
-    xy[1].start()
-    uz.get_late()
-    uy[1].start()
-    xy[0].forward()
-    xz.get_across()
-    ez.forward()
-    ez.near()
-    ex[0].start()
-    ex[1].start()
-    uy[0].forward()
-    uz.get_across()
-    xz.finish()
-    xy[2].start()
-    cz.start()
-    ez.finish()
-    ex[2].start()
-    xy[1].forward()
-    uz.finish()
-    uy[2].start()
-    ex[0].forward()
-    ex[1].forward()
-    uy[1].forward()
-    cz.forward()
-    cz.near()
-    cx[0].start()
-    cx[1].start()
-    cz.finish()
-    cx[2].start()
-    ex[2].forward()
-    xy[2].forward()
-    cx[0].forward()
-    cx[1].forward()
-    cx[2].forward()
-    locals_[2].wait()
-    locals_[3].wait()
-    for gather in ex + cx:
-        gather.finish()
-    partials(y)
-    uy[2].forward()
-
-    @pl.loop(0, 2)
-    def _(n):
-        partials((y + 1 + 2 * n) % 4)
-
-    pointwise(y)
-    for gather in xy + uy:
-        gather.finish()
-    partials((y + 2) % 4)
-
-    @pl.loop(0, 3)
-    def _(n):
-        pointwise((y + 1 + 2 * n - n // 2 * 3) % 4)
-
-    @pl.loop(0, 4)
-    def _(slot):
-        for k in range(2):
-            act_copy(k, slot, 1 - c).wait_recv()
-            hid_copy(k, slot).wait_send()
-            act_copy(k, slot, c).wait_send()
+    def hidden_done():
+        @pl.loop(0, 4)
+        def _(slot):
+            for k in range(2):
+                act_copy(k, slot, 1 - c).wait_recv()
+                hid_copy(k, slot).wait_send()
+                act_copy(k, slot, c).wait_send()
 
     def reduce_to(axis, part_at, inbox, out):
         me, left, right = axis
@@ -467,117 +409,188 @@
         there = ox_ref.at[rows_at(y * 256 + s * 128 + (1 - zl) * 64, 64, 64)]
         net.arrived(chunks[s][3][1], there, beside)
 
-    @pl.loop(0, 4)
-    def _(j):
+    small_k = net.ids(6)
+
+    def grad_expand():
+        @pl.loop(0, 4)
+        def _(j):
+            for h in range(2):
+                acc = (dot(xg[j], ah[1, h], TN) * factor).astype(BF)
+                for q in range(4):
+                    ge[q, j, :, pl.ds(h * 256, 256)] = acc[q * 128:(q + 1) * 128]
+
+    def grad_contract():
+        @pl.loop(0, 4)
+        def _(j):
+            for h in range(2):
+                acc = (dot(ah[0, h], ug[j], TN) * factor).astype(BF)
+                gc[2 * h, j] = acc[:128]
+                gc[2 * h + 1, j] = acc[128:]
+
+    def grad_tokens(s):
+        @pl.loop(0, 4)
+        def _(j):
+            first = ah[1, 0].reshape(4, 2, 128, 256)[:, s].reshape(512, 256)
+            second = ah[1, 1].reshape(4, 2, 128, 256)[:, s].reshape(512, 256)
+            acc = dot(first, eg[j, :, pl.ds(0, 256)], NT) + dot(second, eg[j, :, pl.ds(256, 256)], NT)
+            acc = acc.astype(BF)
+            for slot in range(4):
+                gx[s, slot, j] = acc[slot * 128:(slot + 1) * 128]
+
+    def token_sums():
         for h in range(2):
-            acc = (dot(xg[j], ah[1, h], TN) * factor).astype(BF)
-            for q in range(4):
-                ge[q, j, :, pl.ds(h * 256, 256)] = acc[q * 128:(q + 1) * 128]
-
+            def add_rows(n, acc):
+                block = ah[1, h, rows_at(n * 64, 64, 64)].astype(F32)
+                return acc + jnp.sum(block.reshape(8, 8, 256), axis=0)
+            acc = lax.fori_loop(0, 16, add_rows, jnp.zeros((8, 256), F32))
+            acc = jnp.sum(acc, axis=0, keepdims=True) * factor
+            small[pl.ds(0, 8), pl.ds(h * 256, 256)] = jnp.broadcast_to(acc.astype(BF).astype(F32), (8, 256))
+
+        def add_up(n, acc):
+            block = ug[zh, rows_at(n * 64, 64, 64)].astype(F32)
+            return acc + jnp.sum(block.reshape(8, 8, 512), axis=0)
+        acc = lax.fori_loop(0, 16, add_up, jnp.zeros((8, 512), F32))
+        acc = jnp.sum(acc, axis=0, keepdims=True) * factor
+        small[pl.ds(8, 8)] = jnp.broadcast_to(acc.astype(BF).astype(F32), (8, 512))
+        for n, peer in enumerate((x_right, x_left, x_across)):
+            net.send(small_k[n], small, small_in.at[n], peer)
+
+    def small_sums():
+        for n, peer in enumerate((x_left, x_right, x_across)):
+            net.arrived(small_k[n], small_in.at[n], peer)
+        whole = ((small[...] + small_in[0]) + small_in[1]) + small_in[2]
+        ob_ref[zh] = whole[:8]
+        oo_ref[...] = whole[8:]
+        for n, peer in enumerate((z_right, z_left, z_across)):
+            net.send(small_k[3 + n], ob_ref.at[zh], ob_ref.at[zh], peer)
+
+    locals_[0].wait()
+    xz.start()
+    locals_[1].wait()
+    uz.start()
+    xz.get_early()
+    xy[0].start()
+    ez.start()
+    uz.get_early()
+    uy[0].start()
+    xy[0].forward()
+    uy[0].forward()
+    ez.near()
+    ex[0].start()
+    ex[1].start()
+    xz.get_late()
+    xy[1].start()
+    ez.forward()
+    cz.start()
+    uz.get_late()
+    uy[1].start()
+    xy[1].forward()
+    ez.finish()
+    ex[2].start()
+    ex[2].forward()
+    xz.get_across()
+    cz.forward()
+    ex[0].forward()
+    ex[1].forward()
+    uy[1].forward()
+    cz.near()
+    cx[0].start()
+    cx[1].start()
+    xz.finish()
+    xy[2].start()
+    uz.get_across()
+    cz.finish()
+    cx[2].start()
+    uz.finish()
+    uy[2].start()
+    cx[0].forward()
+    cx[1].forward()
+    cx[2].forward()
+    xy[2].forward()
+    uy[2].forward()
+    locals_[2].wait()
+    locals_[3].wait()
+    for gather in ex + cx:
+        gather.finish()
+    partials((y + 1) % 4)
+    partials((y + 3) % 4)
+    partials(y)
+    for gather in xy + uy:
+        gather.finish()
+    partials((y + 2) % 4)
+    pointwise((y + 1) % 4)
+    pointwise((y + 3) % 4)
+    pointwise(y)
+    pointwise((y + 2) % 4)
+    hidden_done()
+    grad_tokens(0)
+    chunks[0][0].far()
+    grad_expand()
     e_red.far()
+    chunks[0][0].near()
+    grad_tokens(1)
+    chunks[0][0].join()
+    chunks[1][0].far()
     e_red.near()
-    for s in range(2):
-        @pl.loop(0, 4)
-        def _(slot):
-            where = rows_at(slot * 256 + s * 128, 128, 128)
-            for j in range(4):
-                acc = dot(ah[1, 0, where], eg[j, :, pl.ds(0, 256)], NT)
-                acc = acc + dot(ah[1, 1, where], eg[j, :, pl.ds(256, 256)], NT)
-                gx[s, slot, j] = acc.astype(BF)
-        chunks[s][0].far()
-        if s == 0:
-            chunks[s][0].near()
+    chunks[1][0].near()
+    grad_contract()
     e_red.join()
-
-    @pl.loop(0, 4)
-    def _(j):
-        for h in range(2):
-            acc = (dot(ah[0, h], ug[j], TN) * factor).astype(BF)
-            gc[2 * h, j] = acc[:128]
-            gc[2 * h + 1, j] = acc[128:]
-
     c_red.far()
-    c_red.near()
-    chunks[0][0].join()
-    chunks[1][0].near()
-
-    for h in range(2):
-        def add_rows(n, acc):
-            block = ah[1, h, rows_at(n * 64, 64, 64)].astype(F32)
-            return acc + jnp.sum(block.reshape(8, 8, 256), axis=0)
-        acc = lax.fori_loop(0, 16, add_rows, jnp.zeros((8, 256), F32))
-        acc = jnp.sum(acc, axis=0, keepdims=True) * factor
-        small[pl.ds(0, 8), pl.ds(h * 256, 256)] = jnp.broadcast_to(acc.astype(BF).astype(F32), (8, 256))
-
-    def add_up(n, acc):
-        block = ug[zh, rows_at(n * 64, 64, 64)].astype(F32)
-        return acc + jnp.sum(block.reshape(8, 8, 512), axis=0)
-    acc = lax.fori_loop(0, 16, add_up, jnp.zeros((8, 512), F32))
-    acc = jnp.sum(acc, axis=0, keepdims=True) * factor
-    small[pl.ds(8, 8)] = jnp.broadcast_to(acc.astype(BF).astype(F32), (8, 512))
-    small_k = net.ids(6)
-    for n, peer in enumerate((x_right, x_left, x_across)):
-        net.send(small_k[n], small, small_in.at[n], peer)
-
-    e_red.finish()
-    e_swap.start()
-    oe_ref[rows_at(x * 128, 128, 128), rows_at(zh * 512, 512, 512)] = sum_e[zh]
-    e_out[0].start()
-    chunks[1][0].join()
-    c_red.join()
-    e_swap.forward()
     chunks[0][0].finish()
     pair_send(0)
-    for n, peer in enumerate((x_left, x_right, x_across)):
-        net.arrived(small_k[n], small_in.at[n], peer)
-    whole = ((small[...] + small_in[0]) + small_in[1]) + small_in[2]
-    ob_ref[zh] = whole[:8]
-    oo_ref[...] = whole[8:]
-    for n, peer in enumerate((z_right, z_left, z_across)):
-        net.send(small_k[3 + n], ob_ref.at[zh], ob_ref.at[zh], peer)
+    e_red.finish()
+    oe_ref[rows_at(x * 128, 128, 128), rows_at(zh * 512, 512, 512)] = sum_e[zh]
+    e_swap.start()
+    c_red.near()
+    chunks[1][0].join()
+    pair_add(0)
+    chunks[0][1].far()
+    chunks[0][1].near()
+    c_red.join()
+    e_out[0].start()
+    chunks[1][0].finish()
+    pair_send(1)
+    c_red.finish()
+    oc_ref[rows_at(zh * 512 + x * 128, 128, 128)] = sum_c[zh]
+    c_out[0].start()
+    e_out[0].forward()
+    c_swap.start()
+    token_sums()
+    pair_add(1)
+    chunks[1][1].far()
+    chunks[1][1].near()
+    chunks[0][1].join()
     e_swap.near()
     e_out[1].start()
     e_out[2].start()
-    pair_add(0)
-    chunks[0][1].far()
-    chunks[0][1].near()
-    e_swap.finish()
-    e_out[3].start()
-    c_red.finish()
-    c_swap.start()
-    oc_ref[rows_at(zh * 512 + x * 128, 128, 128)] = sum_c[zh]
-    c_out[0].start()
-    chunks[1][0].finish()
-    pair_send(1)
-    chunks[0][1].join()
-    e_out[0].forward()
-    c_swap.forward()
-    chunks[0][1].finish()
-    pair_back(0)
-    pair_add(1)
-    chunks[1][1].far()
-    chunks[1][1].near()
-    e_out[1].forward()
+    c_out[0].forward()
     e_out[2].forward()
-    pair_got(0)
-    chunks[0][2].start()
+    e_swap.forward()
     c_swap.near()
     c_out[1].start()
     c_out[2].start()
     chunks[1][1].join()
-    e_out[3].forward()
+    e_out[1].forward()
+    chunks[0][1].finish()
+    pair_back(0)
+    c_swap.forward()
+    e_swap.finish()
+    e_out[3].start()
+    chunks[1][1].finish()
+    pair_back(1)
+    pair_got(0)
+    chunks[0][2].start()
+    c_out[2].forward()
     c_swap.finish()
     c_out[3].start()
-    chunks[1][1].finish()
-    pair_back(1)
-    c_out[0].forward()
-    chunks[0][2].forward()
+    small_sums()
+    c_out[1].forward()
     pair_got(1)
     chunks[1][2].start()
-    c_out[1].forward()
-    c_out[2].forward()
+    chunks[0][2].forward()
+    e_out[3].forward()
+    c_out[3].forward()
     chunks[1][2].forward()
-    c_out[3].forward()
     for gather in e_out + c_out:
         gather.finish()
     for chunk in chunks:

time: 176 us -> 166 us (0.943)
  Pallas kernels: 175 us -> 165 us
    pallas_call x1, Pallas kernels: 172 us -> 162 us  [local(): pl.pallas_call(kernel, out_shape=(pltpu.VMEM((1024, 512), BF), pltpu.VMEM...]
where the time goes in v3:
time: 166 us
  Pallas kernels  165 us (99%)
    pallas_call x1, Pallas kernels, local(): pl.pallas_call(kernel, out_shape=(pltpu.VMEM((1024, 512), BF), pltpu.VMEM...  162 us

profile of v3, /device:TPU:8, one launch (start us, length us, event | category | flops | bytes accessed | tf_op | source)
XLA Modules:
  0.0 165.8 jit_solution(348862990587652528)
XLA Ops:
  0.6 162.2 %shard_map.92 = (bf16[1024,512]{1,0:T(8,128)(2,1)S(1)}, bf16[512,2048]{1,0:T(8,128)(2,1)S(1)}, f32[4,8,512]{2,1,0:T(8,128)S(1)}, bf16[2048,512]{1,0:T(8,128)(2,1)S(1)}, f32[8,512]{1,0:T(8,128)S(1)}) custom-call(bf16[1024,512]{1,0:T(8,128)(2,1)} %x_ref.1, bf16[1024,512]{1,0:T(8,128)(2,1)} %u_ref.1, bf16[512,2048]{1,0:T(8,128)(2,1)} %e_ref.1, ...), custom_call_target="tpu_custom_call" | custom-call | tf_op jit(solution)/shard_map/pallas_call | solution.py:625
  162.8 3.0 %shard_map.93 = (bf16[1024,512]{1,0:T(8,128)(2,1)}, bf16[512,2048]{1,0:T(8,128)(2,1)}, bf16[16,128]{1,0:T(8,128)(2,1)}, bf16[2048,512]{1,0:T(8,128)(2,1)}, bf16[4,128]{1,0:T(4,128)(2,1)}) custom-call(bf16[1024,512]{1,0:T(8,128)(2,1)S(1)} %get-tuple-element.15.ox, bf16[512,2048]{1,0:T(8,128)(2,1)S(1)} %get-tuple-element.16.oe, ...), custom_call_target="tpu_custom_call" | custom-call | tf_op jit(solution)/shard_map/pallas_call | solution.py:674

commit v4 on v3

--- a/solution.py
+++ b/solution.py
@@ -216,7 +216,7 @@
     ox_ref, oe_ref, ob_ref, oc_ref, oo_ref,
     xg, ug, eg, cg, part, got, ah, relay_e, relay_c,
     ge, gc, gx, in_e, in_c, in_x, sum_e, sum_c, sum_x, relay_ge, relay_gc,
-    pair_in, pair_sum, in_z, small, small_in,
+    pair_in, pair_sum, in_z, small, small_in, slope,
     send_sem, recv_sem, local_sem, hid_send, hid_recv, act_send, act_recv,
 ):
     row, col, x = lax.axis_index("row"), lax.axis_index("col"), lax.axis_index("dp")
@@ -301,7 +301,7 @@
             device_id=twin, device_id_type=MESH,
         )
 
-    def partials(slot):
+    def forward_part(slot):
         where = rows_at(slot * 256, 256, 256)
 
         @pl.loop(0, 2)
@@ -311,17 +311,24 @@
             for j in range(1, 4):
                 acc = acc + dot(xg[j, where], eg[j, :, cols], NN)
             part[0, slot, half] = acc
+
+        hid_copy(0, slot).start()
+
+    def back_part(slot):
+        where = rows_at(slot * 256, 256, 256)
+
+        @pl.loop(0, 2)
+        def _(half):
+            cols = rows_at(half * 256, 256, 256)
             acc = dot(ug[0, where], cg[0, cols], NT)
             for j in range(1, 4):
                 acc = acc + dot(ug[j, where], cg[j, cols], NT)
             part[1, slot, half] = acc
 
-        hid_copy(0, slot).start()
         hid_copy(1, slot).start()
 
-    def pointwise(slot):
+    def activate(slot):
         hid_copy(0, slot).wait_recv()
-        hid_copy(1, slot).wait_recv()
         bias = b_ref[row]
 
         @pl.loop(0, 8)
@@ -329,26 +336,32 @@
             rows = rows_at(r * 32, 32, 32)
             pre = part[0, slot, c, rows] + got[0, slot, rows] + bias
             v = pre.astype(BF).astype(F32)
-            back = (part[1, slot, c, rows] + got[1, slot, rows]).astype(BF).astype(F32)
             k0, k1 = 0.7978845608028654, 0.044715
             sq = v * v
             t = jnp.tanh(k0 * (v + k1 * (sq * v)))
             half = 0.5 * (1.0 + t)
-            slope = half + (0.5 * v) * (1.0 - t * t) * (k0 * (1.0 + 3.0 * k1 * sq))
-            out = rows_at(slot * 256 + r * 32, 32, 32)
-            ah[0, c, out] = (v * half).astype(BF)
-            ah[1, c, out] = (back * slope).astype(BF)
+            slope[slot, rows] = half + (0.5 * v) * (1.0 - t * t) * (k0 * (1.0 + 3.0 * k1 * sq))
+            ah[0, c, rows_at(slot * 256 + r * 32, 32, 32)] = (v * half).astype(BF)
 
         act_copy(0, slot, c).start()
+
+    def multiply(slot):
+        hid_copy(1, slot).wait_recv()
+
+        @pl.loop(0, 4)
+        def _(r):
+            rows = rows_at(r * 64, 64, 64)
+            back = (part[1, slot, c, rows] + got[1, slot, rows]).astype(BF).astype(F32)
+            ah[1, c, rows_at(slot * 256 + r * 64, 64, 64)] = (back * slope[slot, rows]).astype(BF)
+
         act_copy(1, slot, c).start()
 
-    def hidden_done():
+    def swapped(k):
         @pl.loop(0, 4)
         def _(slot):
-            for k in range(2):
-                act_copy(k, slot, 1 - c).wait_recv()
-                hid_copy(k, slot).wait_send()
-                act_copy(k, slot, c).wait_send()
+            act_copy(k, slot, 1 - c).wait_recv()
+            hid_copy(k, slot).wait_send()
+            act_copy(k, slot, c).wait_send()
 
     def reduce_to(axis, part_at, inbox, out):
         me, left, right = axis
@@ -470,127 +483,140 @@
     uz.start()
     xz.get_early()
     xy[0].start()
-    ez.start()
     uz.get_early()
     uy[0].start()
-    xy[0].forward()
+    xz.get_late()
+    xy[1].start()
+    ez.start()
+    xz.get_across()
     uy[0].forward()
+    ez.forward()
+    uz.get_late()
+    uy[1].start()
+    cz.start()
+    xy[1].forward()
     ez.near()
     ex[0].start()
     ex[1].start()
-    xz.get_late()
-    xy[1].start()
-    ez.forward()
-    cz.start()
-    uz.get_late()
-    uy[1].start()
-    xy[1].forward()
+    xz.finish()
+    xy[2].start()
+    xy[0].forward()
     ez.finish()
     ex[2].start()
-    ex[2].forward()
-    xz.get_across()
-    cz.forward()
     ex[0].forward()
     ex[1].forward()
-    uy[1].forward()
+    uz.get_across()
+    ex[2].forward()
+    xy[2].forward()
     cz.near()
     cx[0].start()
     cx[1].start()
-    xz.finish()
-    xy[2].start()
-    uz.get_across()
+    cz.forward()
+    locals_[2].wait()
+    for gather in ex:
+        gather.finish()
+    uz.finish()
+    uy[2].start()
+    uy[1].forward()
+    forward_part((y + 1) % 4)
+    forward_part(y)
+    forward_part((y + 3) % 4)
+    for gather in xy:
+        gather.finish()
+    forward_part((y + 2) % 4)
     cz.finish()
     cx[2].start()
-    uz.finish()
-    uy[2].start()
+    activate(y)
     cx[0].forward()
     cx[1].forward()
+    activate((y + 2) % 4)
+    uy[2].forward()
+    activate((y + 1) % 4)
+    activate((y + 3) % 4)
     cx[2].forward()
-    xy[2].forward()
-    uy[2].forward()
-    locals_[2].wait()
     locals_[3].wait()
-    for gather in ex + cx:
+    for gather in cx:
         gather.finish()
-    partials((y + 1) % 4)
-    partials((y + 3) % 4)
-    partials(y)
-    for gather in xy + uy:
+    swapped(0)
+    for gather in uy:
         gather.finish()
-    partials((y + 2) % 4)
-    pointwise((y + 1) % 4)
-    pointwise((y + 3) % 4)
-    pointwise(y)
-    pointwise((y + 2) % 4)
-    hidden_done()
+    back_part((y + 2) % 4)
+    grad_contract()
+    c_red.far()
+    back_part((y + 1) % 4)
+    back_part((y + 3) % 4)
+    back_part(y)
+    multiply((y + 1) % 4)
+    multiply(y)
+    multiply((y + 3) % 4)
+    c_red.near()
+    multiply((y + 2) % 4)
+    swapped(1)
+    grad_tokens(1)
+    chunks[1][0].far()
+    c_red.join()
     grad_tokens(0)
-    chunks[0][0].far()
+    chunks[1][0].near()
     grad_expand()
     e_red.far()
+    chunks[1][0].join()
+    e_red.near()
+    chunks[0][0].far()
+    c_red.finish()
+    oc_ref[rows_at(zh * 512 + x * 128, 128, 128)] = sum_c[zh]
+    c_swap.start()
+    c_swap.forward()
     chunks[0][0].near()
-    grad_tokens(1)
-    chunks[0][0].join()
-    chunks[1][0].far()
-    e_red.near()
-    chunks[1][0].near()
-    grad_contract()
     e_red.join()
-    c_red.far()
-    chunks[0][0].finish()
-    pair_send(0)
+    chunks[1][0].finish()
+    pair_send(1)
+    c_swap.finish()
+    c_out[3].start()
+    c_out[0].start()
     e_red.finish()
     oe_ref[rows_at(x * 128, 128, 128), rows_at(zh * 512, 512, 512)] = sum_e[zh]
     e_swap.start()
-    c_red.near()
-    chunks[1][0].join()
+    chunks[0][0].join()
+    pair_add(1)
+    chunks[1][1].far()
+    chunks[1][1].near()
+    c_swap.near()
+    c_out[1].start()
+    c_out[2].start()
+    chunks[0][0].finish()
+    pair_send(0)
+    token_sums()
+    e_out[0].start()
+    e_swap.near()
+    e_out[1].start()
+    e_out[2].start()
+    e_out[0].forward()
+    chunks[1][1].join()
     pair_add(0)
     chunks[0][1].far()
     chunks[0][1].near()
-    c_red.join()
-    e_out[0].start()
-    chunks[1][0].finish()
-    pair_send(1)
-    c_red.finish()
-    oc_ref[rows_at(zh * 512 + x * 128, 128, 128)] = sum_c[zh]
-    c_out[0].start()
-    e_out[0].forward()
-    c_swap.start()
-    token_sums()
-    pair_add(1)
-    chunks[1][1].far()
-    chunks[1][1].near()
+    e_out[1].forward()
+    chunks[1][1].finish()
+    pair_back(1)
     chunks[0][1].join()
-    e_swap.near()
-    e_out[1].start()
-    e_out[2].start()
-    c_out[0].forward()
+    e_swap.forward()
     e_out[2].forward()
-    e_swap.forward()
-    c_swap.near()
-    c_out[1].start()
-    c_out[2].start()
-    chunks[1][1].join()
-    e_out[1].forward()
+    c_out[2].forward()
     chunks[0][1].finish()
     pair_back(0)
-    c_swap.forward()
-    e_swap.finish()
-    e_out[3].start()
-    chunks[1][1].finish()
-    pair_back(1)
-    pair_got(0)
-    chunks[0][2].start()
-    c_out[2].forward()
-    c_swap.finish()
-    c_out[3].start()
-    small_sums()
     c_out[1].forward()
     pair_got(1)
     chunks[1][2].start()
+    e_swap.finish()
+    e_out[3].start()
+    small_sums()
+    c_out[3].forward()
+    c_out[0].forward()
+    pair_got(0)
+    chunks[0][2].start()
+    chunks[1][2].forward()
+    e_out[3].forward()
     chunks[0][2].forward()
-    e_out[3].forward()
-    c_out[3].forward()
-    chunks[1][2].forward()
     for gather in e_out + c_out:
         gather.finish()
     for chunk in chunks:
@@ -659,6 +685,7 @@
             pltpu.VMEM((2, 6, 32, 512), BF),
             pltpu.VMEM((16, 512), F32),
             pltpu.VMEM((3, 16, 512), F32),
+            pltpu.VMEM((4, 256, 256), F32),
             dma((224,)),
             dma((224,)),
             dma((4,)),

time: 166 us -> 162 us (0.976)
  Pallas kernels: 165 us -> 160 us
    pallas_call x1, Pallas kernels: 162 us -> 157 us  [local(): pl.pallas_call(kernel, out_shape=(pltpu.VMEM((1024, 512), BF), pltpu.VMEM...]
where the time goes in v4:
time: 162 us; the launch traced here: 161 us
  Pallas kernels  160 us (99%)
    pallas_call x1, Pallas kernels, local(): pl.pallas_call(kernel, out_shape=(pltpu.VMEM((1024, 512), BF), pltpu.VMEM...  157 us

profile of v4, /device:TPU:8, one launch (start us, length us, event | category | flops | bytes accessed | tf_op | source)
XLA Modules:
  0.0 160.7 jit_solution(16812085386447217963)
XLA Ops:
  0.6 157.1 %shard_map.92 = (bf16[1024,512]{1,0:T(8,128)(2,1)S(1)}, bf16[512,2048]{1,0:T(8,128)(2,1)S(1)}, f32[4,8,512]{2,1,0:T(8,128)S(1)}, bf16[2048,512]{1,0:T(8,128)(2,1)S(1)}, f32[8,512]{1,0:T(8,128)S(1)}) custom-call(bf16[1024,512]{1,0:T(8,128)(2,1)} %x_ref.1, bf16[1024,512]{1,0:T(8,128)(2,1)} %u_ref.1, bf16[512,2048]{1,0:T(8,128)(2,1)} %e_ref.1, ...), custom_call_target="tpu_custom_call" | custom-call | tf_op jit(solution)/shard_map/pallas_call | solution.py:651
  157.7 3.0 %shard_map.93 = (bf16[1024,512]{1,0:T(8,128)(2,1)}, bf16[512,2048]{1,0:T(8,128)(2,1)}, bf16[16,128]{1,0:T(8,128)(2,1)}, bf16[2048,512]{1,0:T(8,128)(2,1)}, bf16[4,128]{1,0:T(4,128)(2,1)}) custom-call(bf16[1024,512]{1,0:T(8,128)(2,1)S(1)} %get-tuple-element.15.ox, bf16[512,2048]{1,0:T(8,128)(2,1)S(1)} %get-tuple-element.16.oe, ...), custom_call_target="tpu_custom_call" | custom-call | tf_op jit(solution)/shard_map/pallas_call | solution.py:701

commit v5 on v4

--- a/solution.py
+++ b/solution.py
@@ -225,7 +225,6 @@
     factor = 1.0 / 64.0
 
     z_right, z_left = {"row": ((zh + 1) % 4) * 2 + c}, {"row": ((zh + 3) % 4) * 2 + c}
-    z_across = {"row": ((zh + 2) % 4) * 2 + c}
     y_right, y_left = {"col": ((y + 1) % 4) * 2 + zl}, {"col": ((y + 3) % 4) * 2 + zl}
     x_right, x_left, x_across = {"dp": (x + 1) % 4}, {"dp": (x + 3) % 4}, {"dp": (x + 2) % 4}
     twin = {"row": zh * 2 + 1 - c}
@@ -242,7 +241,7 @@
         copy.start()
 
     barrier = pltpu.get_barrier_semaphore()
-    peers = (z_right, z_left, z_across, y_right, y_left, x_right, x_left, x_across, twin, beside, outer)
+    peers = (z_right, z_left, y_right, y_left, x_right, x_left, x_across, twin, beside, outer)
     for peer in peers:
         pl.semaphore_signal(barrier, inc=1, device_id=peer, device_id_type=MESH)
     pl.semaphore_wait(barrier, len(peers))
@@ -314,18 +313,24 @@
 
         hid_copy(0, slot).start()
 
-    def back_part(slot):
-        where = rows_at(slot * 256, 256, 256)
+    def back_half(half):
+        cols = rows_at(half * 256, 256, 256)
 
         @pl.loop(0, 2)
-        def _(half):
-            cols = rows_at(half * 256, 256, 256)
+        def _(n):
+            where = rows_at(n * 512, 512, 512)
             acc = dot(ug[0, where], cg[0, cols], NT)
             for j in range(1, 4):
                 acc = acc + dot(ug[j, where], cg[j, cols], NT)
-            part[1, slot, half] = acc
-
-        hid_copy(1, slot).start()
+            part[1, 2 * n, half] = acc[:256]
+            part[1, 2 * n + 1, half] = acc[256:]
+
+    def back_theirs():
+        back_half(1 - c)
+
+        @pl.loop(0, 4)
+        def _(slot):
+            hid_copy(1, slot).start()
 
     def activate(slot):
         hid_copy(0, slot).wait_recv()
@@ -474,8 +479,13 @@
         whole = ((small[...] + small_in[0]) + small_in[1]) + small_in[2]
         ob_ref[zh] = whole[:8]
         oo_ref[...] = whole[8:]
-        for n, peer in enumerate((z_right, z_left, z_across)):
+        for n, peer in enumerate((z_right, z_left)):
             net.send(small_k[3 + n], ob_ref.at[zh], ob_ref.at[zh], peer)
+
+    def small_forward():
+        before = ob_ref.at[(zh + 3) % 4]
+        net.arrived(small_k[3], before, z_left)
+        net.send(small_k[5], before, before, z_right)
 
     locals_[0].wait()
     xz.start()
@@ -487,25 +497,25 @@
     uy[0].start()
     xz.get_late()
     xy[1].start()
+    xy[0].forward()
     ez.start()
-    xz.get_across()
-    uy[0].forward()
-    ez.forward()
     uz.get_late()
     uy[1].start()
-    cz.start()
+    xz.get_across()
     xy[1].forward()
+    ez.forward()
     ez.near()
     ex[0].start()
     ex[1].start()
+    cz.start()
     xz.finish()
     xy[2].start()
-    xy[0].forward()
+    uy[1].forward()
+    uz.get_across()
     ez.finish()
     ex[2].start()
     ex[0].forward()
     ex[1].forward()
-    uz.get_across()
     ex[2].forward()
     xy[2].forward()
     cz.near()
@@ -517,112 +527,111 @@
         gather.finish()
     uz.finish()
     uy[2].start()
-    uy[1].forward()
-    forward_part((y + 1) % 4)
+    uy[0].forward()
     forward_part(y)
     forward_part((y + 3) % 4)
+    cz.finish()
+    cx[2].start()
+    forward_part((y + 1) % 4)
+    activate((y + 3) % 4)
+    cx[0].forward()
+    cx[1].forward()
     for gather in xy:
         gather.finish()
     forward_part((y + 2) % 4)
-    cz.finish()
-    cx[2].start()
+    uy[2].forward()
+    cx[2].forward()
+    activate((y + 2) % 4)
     activate(y)
-    cx[0].forward()
-    cx[1].forward()
-    activate((y + 2) % 4)
-    uy[2].forward()
     activate((y + 1) % 4)
-    activate((y + 3) % 4)
-    cx[2].forward()
+    swapped(0)
     locals_[3].wait()
     for gather in cx:
         gather.finish()
-    swapped(0)
     for gather in uy:
         gather.finish()
-    back_part((y + 2) % 4)
+    back_theirs()
     grad_contract()
     c_red.far()
-    back_part((y + 1) % 4)
-    back_part((y + 3) % 4)
-    back_part(y)
+    back_half(c)
+    multiply((y + 2) % 4)
+    multiply((y + 3) % 4)
+    multiply(y)
+    c_red.near()
     multiply((y + 1) % 4)
-    multiply(y)
-    multiply((y + 3) % 4)
-    c_red.near()
-    multiply((y + 2) % 4)
     swapped(1)
     grad_tokens(1)
     chunks[1][0].far()
+    chunks[1][0].near()
     c_red.join()
+    grad_expand()
+    chunks[1][0].join()
+    e_red.far()
     grad_tokens(0)
-    chunks[1][0].near()
-    grad_expand()
-    e_red.far()
-    chunks[1][0].join()
+    chunks[0][0].far()
+    chunks[0][0].near()
     e_red.near()
-    chunks[0][0].far()
     c_red.finish()
     oc_ref[rows_at(zh * 512 + x * 128, 128, 128)] = sum_c[zh]
     c_swap.start()
     c_swap.forward()
-    chunks[0][0].near()
     e_red.join()
+    c_out[0].start()
     chunks[1][0].finish()
     pair_send(1)
-    c_swap.finish()
-    c_out[3].start()
-    c_out[0].start()
+    chunks[0][0].join()
     e_red.finish()
     oe_ref[rows_at(x * 128, 128, 128), rows_at(zh * 512, 512, 512)] = sum_e[zh]
     e_swap.start()
-    chunks[0][0].join()
+    e_out[0].start()
+    token_sums()
     pair_add(1)
     chunks[1][1].far()
     chunks[1][1].near()
+    chunks[0][0].finish()
+    pair_send(0)
     c_swap.near()
     c_out[1].start()
     c_out[2].start()
-    chunks[0][0].finish()
-    pair_send(0)
-    token_sums()
-    e_out[0].start()
+    c_swap.finish()
+    c_out[3].start()
+    c_out[1].forward()
+    c_out[3].forward()
+    chunks[1][1].join()
+    c_out[0].forward()
     e_swap.near()
     e_out[1].start()
     e_out[2].start()
     e_out[0].forward()
-    chunks[1][1].join()
+    c_out[2].forward()
     pair_add(0)
     chunks[0][1].far()
     chunks[0][1].near()
-    e_out[1].forward()
     chunks[1][1].finish()
     pair_back(1)
     chunks[0][1].join()
+    e_out[1].forward()
     e_swap.forward()
-    e_out[2].forward()
-    c_out[2].forward()
     chunks[0][1].finish()
     pair_back(0)
-    c_out[1].forward()
     pair_got(1)
     chunks[1][2].start()
     e_swap.finish()
     e_out[3].start()
+    e_out[2].forward()
     small_sums()
-    c_out[3].forward()
-    c_out[0].forward()
     pair_got(0)
     chunks[0][2].start()
     chunks[1][2].forward()
     e_out[3].forward()
+    small_forward()
     chunks[0][2].forward()
     for gather in e_out + c_out:
         gather.finish()
     for chunk in chunks:
         chunk[2].finish()
-    for n, d in enumerate((3, 1, 2)):
-        net.arrived(small_k[3 + n], ob_ref.at[(zh + d) % 4], z_across)
+    net.arrived(small_k[4], ob_ref.at[(zh + 1) % 4], z_right)
+    net.arrived(small_k[5], ob_ref.at[(zh + 2) % 4], z_left)
     net.drain()
     assert net.used <= 224
 

time: 162 us -> 158 us (0.975)
  Pallas kernels: 160 us -> 157 us
    pallas_call x1, Pallas kernels: 157 us -> 154 us  [local(): pl.pallas_call(kernel, out_shape=(pltpu.VMEM((1024, 512), BF), pltpu.VMEM...]
where the time goes in v5:
time: 158 us
  Pallas kernels  157 us (99%)
    pallas_call x1, Pallas kernels, local(): pl.pallas_call(kernel, out_shape=(pltpu.VMEM((1024, 512), BF), pltpu.VMEM...  154 us

profile of v5, /device:TPU:8, one launch (start us, length us, event | category | flops | bytes accessed | tf_op | source)
XLA Modules:
  0.0 157.7 jit_solution(5946651811446795399)
XLA Ops:
  0.6 154.1 %shard_map.92 = (bf16[1024,512]{1,0:T(8,128)(2,1)S(1)}, bf16[512,2048]{1,0:T(8,128)(2,1)S(1)}, f32[4,8,512]{2,1,0:T(8,128)S(1)}, bf16[2048,512]{1,0:T(8,128)(2,1)S(1)}, f32[8,512]{1,0:T(8,128)S(1)}) custom-call(bf16[1024,512]{1,0:T(8,128)(2,1)} %x_ref.1, bf16[1024,512]{1,0:T(8,128)(2,1)} %u_ref.1, bf16[512,2048]{1,0:T(8,128)(2,1)} %e_ref.1, ...), custom_call_target="tpu_custom_call" | custom-call | tf_op jit(solution)/shard_map/pallas_call | solution.py:660
  154.8 3.0 %shard_map.93 = (bf16[1024,512]{1,0:T(8,128)(2,1)}, bf16[512,2048]{1,0:T(8,128)(2,1)}, bf16[16,128]{1,0:T(8,128)(2,1)}, bf16[2048,512]{1,0:T(8,128)(2,1)}, bf16[4,128]{1,0:T(4,128)(2,1)}) custom-call(bf16[1024,512]{1,0:T(8,128)(2,1)S(1)} %get-tuple-element.15.ox, bf16[512,2048]{1,0:T(8,128)(2,1)S(1)} %get-tuple-element.16.oe, ...), custom_call_target="tpu_custom_call" | custom-call | tf_op jit(solution)/shard_map/pallas_call | solution.py:710

commit v6 on v5

--- a/solution.py
+++ b/solution.py
@@ -142,7 +142,7 @@
 
 
 def add_into(target, other):
-    rows = min(64, target.shape[-2])
+    rows = min(128, target.shape[-2])
     lead = target.shape[0] if len(target.shape) == 3 else 1
     depth = target.shape[-2]
 
@@ -158,7 +158,7 @@
 
 
 def total_into(out, parts):
-    rows = min(64, out.shape[-2])
+    rows = min(128, out.shape[-2])
     lead = out.shape[0] if len(out.shape) == 3 else 1
     depth = out.shape[-2]
 
@@ -437,13 +437,12 @@
                 for q in range(4):
                     ge[q, j, :, pl.ds(h * 256, 256)] = acc[q * 128:(q + 1) * 128]
 
-    def grad_contract():
+    def grad_contract(h):
         @pl.loop(0, 4)
         def _(j):
-            for h in range(2):
-                acc = (dot(ah[0, h], ug[j], TN) * factor).astype(BF)
-                gc[2 * h, j] = acc[:128]
-                gc[2 * h + 1, j] = acc[128:]
+            acc = (dot(ah[0, h], ug[j], TN) * factor).astype(BF)
+            gc[2 * h, j] = acc[:128]
+            gc[2 * h + 1, j] = acc[128:]
 
     def grad_tokens(s):
         @pl.loop(0, 4)
@@ -495,29 +494,29 @@
     xy[0].start()
     uz.get_early()
     uy[0].start()
+    xy[0].forward()
     xz.get_late()
     xy[1].start()
-    xy[0].forward()
     ez.start()
+    xz.get_across()
     uz.get_late()
     uy[1].start()
-    xz.get_across()
-    xy[1].forward()
-    ez.forward()
     ez.near()
     ex[0].start()
     ex[1].start()
-    cz.start()
+    ez.forward()
     xz.finish()
     xy[2].start()
-    uy[1].forward()
-    uz.get_across()
+    cz.start()
     ez.finish()
     ex[2].start()
     ex[0].forward()
     ex[1].forward()
+    uy[1].forward()
+    xy[2].forward()
     ex[2].forward()
-    xy[2].forward()
+    xy[1].forward()
+    uz.get_across()
     cz.near()
     cx[0].start()
     cx[1].start()
@@ -525,106 +524,107 @@
     locals_[2].wait()
     for gather in ex:
         gather.finish()
+    forward_part((y + 3) % 4)
     uz.finish()
     uy[2].start()
+    forward_part((y + 1) % 4)
     uy[0].forward()
     forward_part(y)
-    forward_part((y + 3) % 4)
     cz.finish()
     cx[2].start()
-    forward_part((y + 1) % 4)
+    activate(y)
+    activate((y + 1) % 4)
+    for gather in xy:
+        gather.finish()
+    forward_part((y + 2) % 4)
     activate((y + 3) % 4)
     cx[0].forward()
     cx[1].forward()
-    for gather in xy:
+    uy[2].forward()
+    activate((y + 2) % 4)
+    cx[2].forward()
+    swapped(0)
+    for gather in uy:
         gather.finish()
-    forward_part((y + 2) % 4)
-    uy[2].forward()
-    cx[2].forward()
-    activate((y + 2) % 4)
-    activate(y)
-    activate((y + 1) % 4)
-    swapped(0)
+    grad_contract((x + 2) % 4 // 2)
+    c_red.far()
     locals_[3].wait()
     for gather in cx:
         gather.finish()
-    for gather in uy:
-        gather.finish()
     back_theirs()
-    grad_contract()
-    c_red.far()
     back_half(c)
+    multiply(y)
+    grad_contract(1 - (x + 2) % 4 // 2)
+    c_red.near()
+    multiply((y + 3) % 4)
     multiply((y + 2) % 4)
-    multiply((y + 3) % 4)
-    multiply(y)
-    c_red.near()
     multiply((y + 1) % 4)
     swapped(1)
     grad_tokens(1)
     chunks[1][0].far()
-    chunks[1][0].near()
     c_red.join()
     grad_expand()
-    chunks[1][0].join()
+    chunks[1][0].near()
     e_red.far()
-    grad_tokens(0)
-    chunks[0][0].far()
-    chunks[0][0].near()
-    e_red.near()
     c_red.finish()
     oc_ref[rows_at(zh * 512 + x * 128, 128, 128)] = sum_c[zh]
     c_swap.start()
+    chunks[1][0].join()
+    e_red.near()
+    grad_tokens(0)
+    chunks[0][0].far()
     c_swap.forward()
     e_red.join()
     c_out[0].start()
+    chunks[0][0].near()
     chunks[1][0].finish()
     pair_send(1)
-    chunks[0][0].join()
     e_red.finish()
     oe_ref[rows_at(x * 128, 128, 128), rows_at(zh * 512, 512, 512)] = sum_e[zh]
     e_swap.start()
-    e_out[0].start()
-    token_sums()
+    chunks[0][0].join()
+    c_swap.finish()
+    c_out[3].start()
     pair_add(1)
     chunks[1][1].far()
     chunks[1][1].near()
-    chunks[0][0].finish()
-    pair_send(0)
     c_swap.near()
     c_out[1].start()
     c_out[2].start()
-    c_swap.finish()
-    c_out[3].start()
+    chunks[0][0].finish()
+    pair_send(0)
+    c_out[0].forward()
+    e_out[0].start()
     c_out[1].forward()
-    c_out[3].forward()
-    chunks[1][1].join()
-    c_out[0].forward()
+    token_sums()
     e_swap.near()
     e_out[1].start()
     e_out[2].start()
     e_out[0].forward()
     c_out[2].forward()
+    chunks[1][1].join()
     pair_add(0)
     chunks[0][1].far()
     chunks[0][1].near()
     chunks[1][1].finish()
     pair_back(1)
+    c_out[3].forward()
     chunks[0][1].join()
     e_out[1].forward()
+    e_out[2].forward()
     e_swap.forward()
+    pair_got(1)
+    chunks[1][2].start()
     chunks[0][1].finish()
     pair_back(0)
-    pair_got(1)
-    chunks[1][2].start()
     e_swap.finish()
     e_out[3].start()
-    e_out[2].forward()
-    small_sums()
     pair_got(0)
     chunks[0][2].start()
+    small_sums()
     chunks[1][2].forward()
+    small_forward()
     e_out[3].forward()
-    small_forward()
     chunks[0][2].forward()
     for gather in e_out + c_out:
         gather.finish()

time: 158 us -> 157 us (level)
  Pallas kernels: 157 us -> 155 us
    pallas_call x1, Pallas kernels: 154 us -> 152 us  [local(): pl.pallas_call(kernel, out_shape=(pltpu.VMEM((1024, 512), BF), pltpu.VMEM...]
where the time goes in v6:
time: 157 us; the launch traced here: 156 us
  Pallas kernels  155 us (99%)
    pallas_call x1, Pallas kernels, local(): pl.pallas_call(kernel, out_shape=(pltpu.VMEM((1024, 512), BF), pltpu.VMEM...  152 us

profile of v6, /device:TPU:8, one launch (start us, length us, event | category | flops | bytes accessed | tf_op | source)
XLA Modules:
  0.0 156.1 jit_solution(5119899017125143290)
XLA Ops:
  0.6 152.5 %shard_map.92 = (bf16[1024,512]{1,0:T(8,128)(2,1)S(1)}, bf16[512,2048]{1,0:T(8,128)(2,1)S(1)}, f32[4,8,512]{2,1,0:T(8,128)S(1)}, bf16[2048,512]{1,0:T(8,128)(2,1)S(1)}, f32[8,512]{1,0:T(8,128)S(1)}) custom-call(bf16[1024,512]{1,0:T(8,128)(2,1)} %x_ref.1, bf16[1024,512]{1,0:T(8,128)(2,1)} %u_ref.1, bf16[512,2048]{1,0:T(8,128)(2,1)} %e_ref.1, ...), custom_call_target="tpu_custom_call" | custom-call | tf_op jit(solution)/shard_map/pallas_call | solution.py:660
  153.1 3.0 %shard_map.93 = (bf16[1024,512]{1,0:T(8,128)(2,1)}, bf16[512,2048]{1,0:T(8,128)(2,1)}, bf16[16,128]{1,0:T(8,128)(2,1)}, bf16[2048,512]{1,0:T(8,128)(2,1)}, bf16[4,128]{1,0:T(4,128)(2,1)}) custom-call(bf16[1024,512]{1,0:T(8,128)(2,1)S(1)} %get-tuple-element.15.ox, bf16[512,2048]{1,0:T(8,128)(2,1)S(1)} %get-tuple-element.16.oe, ...), custom_call_target="tpu_custom_call" | custom-call | tf_op jit(solution)/shard_map/pallas_call | solution.py:710
